TPU v7x, 32 devices: a whole 2x2x4 slice. The times are simulated.
32 devices in a mesh: seq: 8 (over z, y), head: 4 (over x, core).
Axes of the slice: x: 2, y: 2, z: 4, core: 2. Of those that a mesh axis runs over, the one named last changes fastest.
Arguments:
- queries: bfloat16 [4096, 4096], P('seq', 'head'), may hold values from -5 to 5
- keys: bfloat16 [4096, 1024], P('seq', 'head'), may hold values from -5 to 5
- values: bfloat16 [4096, 1024], P('seq', 'head'), may hold values from -5 to 5
- doc_lengths: int32 [16], replicated, may hold values from 1 to 2048, 4096 in all
- out_weight: bfloat16 [4096, 4096], P('head', 'seq'), may hold values from -0.125 to 0.125
Outputs:
- mixed: bfloat16 [4096, 4096], P('seq', 'head')
Inputs may be any that keep to these rules, and one draw needn't show every extreme that they name: `doc_lengths`: the lengths sum to 4096, and one document is exactly 2048 tokens long.
All inputs are finite; a program needn't handle non-finite values.
Results may differ from a plain program's by a relative error of at most 0.012.
Values may be sent and summed in bfloat16 or wider, within the bound.
A program may use at most 128 MiB of HBM per device.

v0:
```python
import functools
import math

import jax
import jax.numpy as jnp
from jax import lax
from jax.experimental import pallas as pl
from jax.experimental.pallas import tpu as pltpu
from jax.sharding import PartitionSpec as P

HQ = 32
KV = 8
DH = 128
MOST = 2048
CHUNKS = 4
MESH = pl.DeviceIdType.MESH


def kernel(
    n_seq, lens_ref, q_ref, k_hbm, v_hbm, w_hbm, out_ref,
    kbuf, vbuf, wbuf, bias, vt, mx, sm, acc, both,
    tmp, keep, sum1, sum2, give3, got3,
    load_sem, kvz_send, kvy_send, kv_recv, wl_send, wl_recv, wr_send, wr_recv,
    at_send, at_recv, s1_send, s1_recv, s2_send, s2_recv, s3_send, s3_recv,
):
    s, h = lax.axis_index("seq"), lax.axis_index("head")
    pairs = n_seq // 2
    p, m = s // 2, lax.rem(s, 2)
    mate = s + 1 - 2 * m
    right = lax.rem(p + 1, pairs) * 2 + m
    left = lax.rem(p + pairs - 1, pairs) * 2 + m
    near = h + 1 - 2 * lax.rem(h, 2)
    far = lax.rem(h + 2, 4)
    rows = q_ref.shape[0]
    depth, wc = w_hbm.shape
    half = depth // 2
    groups = pairs // 4
    group_size = HQ // KV
    part = rows * 2 // CHUNKS
    has_up, has_down = p + 1 < pairs, p >= 1
    scale = DH ** (-0.5) * math.log2(math.e)

    def copy(src, dst, send, recv, seq, head):
        return pltpu.make_async_remote_copy(
            src_ref=src, dst_ref=dst, send_sem=send, recv_sem=recv,
            device_id={"seq": seq, "head": head}, device_id_type=MESH,
        )

    def kv_copies(src_slot, dst_slot, j, send, target):
        cols = pl.ds(pl.multiple_of(j * DH, DH), DH)
        return [
            copy(buf.at[src_slot, :, cols], buf.at[dst_slot, :, cols],
                 send.at[j, c], kv_recv.at[dst_slot, j, c], target, h)
            for c, buf in enumerate((kbuf, vbuf))
        ]

    def w_copy(block, part_at, step, send, recv, target):
        piece = wbuf.at[block, pl.ds(part_at * half, half)]
        return copy(piece, piece, send.at[step, part_at], recv.at[step, part_at], target, h)

    def left_copy(step, part_at):
        return w_copy(jnp.minimum(p + step, pairs - 1), part_at, step, wl_send, wl_recv, left)

    def right_copy(step, part_at):
        return w_copy(jnp.maximum(p - step, 0), part_at, step, wr_send, wr_recv, right)

    loads = [
        pltpu.make_async_copy(k_hbm, kbuf.at[0], load_sem.at[0]),
        pltpu.make_async_copy(v_hbm, vbuf.at[0], load_sem.at[1]),
        pltpu.make_async_copy(w_hbm, wbuf.at[p], load_sem.at[2]),
    ]
    for load in loads:
        load.start()

    barrier = pltpu.get_barrier_semaphore()
    for seq, head in ((mate, h), (left, h), (right, h), (s, near), (s, far)):
        pl.semaphore_signal(barrier, inc=1, device_id={"seq": seq, "head": head}, device_id_type=MESH)
    pl.semaphore_wait(barrier, 5)

    loads[0].wait()
    loads[1].wait()
    has_next = s + 2 < n_seq
    for j in range(2):
        @pl.when(has_next)
        def _():
            for c in kv_copies(0, 2, j, kvz_send.at[0], right):
                c.start()

        @pl.when(m == 0)
        def _():
            for c in kv_copies(0, 1, j, kvy_send.at[0], mate):
                c.start()

    loads[2].wait()

    @pl.when(has_down)
    def _():
        for a in range(2):
            left_copy(0, a).start()

    q_pos = s * rows + lax.broadcasted_iota(jnp.int32, (1, rows), 1)
    start = jnp.int32(0)
    first = jnp.zeros((1, rows), jnp.int32)
    for d in range(1, lens_ref.shape[0]):
        start = start + lens_ref[d - 1]
        first = jnp.where(q_pos >= start, start, first)

    def attn_copy(j):
        return copy(both.at[1, j], both.at[0, j], at_send.at[j], at_recv.at[j], mate, h)

    def finish(j):
        def one(g, _):
            i = j * group_size + g
            full = jnp.transpose(acc[i] / sm[i])
            both[1, j, :, pl.ds(pl.multiple_of(g * DH, DH), DH)] = full.astype(jnp.bfloat16)
            return 0

        lax.fori_loop(0, group_size, one, 0)
        attn_copy(j).start()

    def step(i, _):
        k = jnp.maximum(i - 2, 0)
        w = lax.rem(k, 4)
        slot = jnp.where(i < 2, 0, 2 + 2 * (k // 4) - lax.rem(w, 2))
        j = jnp.where(i < 2, i, w // 2)

        @pl.when((i >= 2) & (s >= slot))
        def _():
            for c in kv_copies(slot, slot, j, kvz_send.at[0], right):
                c.wait_recv()

            @pl.when((slot == 2) & has_next)
            def _():
                for c in kv_copies(2, 4, j, kvz_send.at[1], right):
                    c.start()

            @pl.when(slot == 2)
            def _():
                for c in kv_copies(2, 3 - 2 * m, j, kvy_send.at[1], mate):
                    c.start()

            @pl.when((slot == 4) & (m == 1))
            def _():
                for c in kv_copies(4, 3, j, kvy_send.at[2], mate):
                    c.start()

        @pl.when((i == 4) & has_up)
        def _():
            for a in range(2):
                right_copy(0, a).start()

        for at, a in ((5, 0), (8, 1)):
            @pl.when((i == at) & has_up)
            def _():
                left_copy(0, a).wait_recv()

                @pl.when(has_down)
                def _():
                    left_copy(1, a).start()

        @pl.when(s >= slot)
        def _():
            cols = pl.ds(pl.multiple_of(j * DH, DH), DH)
            k_pos = (s - slot) * rows + lax.broadcasted_iota(jnp.int32, (rows, rows), 0)
            bias[...] = jnp.where((k_pos >= first) & (k_pos <= q_pos), 0.0, -1e30)
            vt[...] = jnp.transpose(vbuf[slot, :, cols])

            def one(g, _):
                at = j * group_size + g
                q = q_ref[:, pl.ds(pl.multiple_of(at * DH, DH), DH)]
                scores = lax.dot_general(
                    kbuf[slot, :, cols], q, (((1,), (1,)), ((), ())),
                    preferred_element_type=jnp.float32,
                ) * scale + bias[...]
                top = jnp.max(scores, axis=0, keepdims=True)
                old = jnp.where(i < 2, jnp.full_like(top, -1e30), mx[at])
                new = jnp.maximum(old, top)
                probs = jnp.exp2(scores - new)
                fade = jnp.exp2(old - new)
                mx[at] = new
                total = jnp.sum(probs, axis=0, keepdims=True)
                sm[at] = jnp.where(i < 2, total, sm[at] * fade + total)
                mixed = jnp.dot(vt[...], probs.astype(jnp.bfloat16), preferred_element_type=jnp.float32)

                @pl.when(i < 2)
                def _():
                    acc[at] = mixed

                @pl.when(i >= 2)
                def _():
                    acc[at] = acc[at] * fade + mixed

                return 0

            lax.fori_loop(0, group_size, one, 0)

        for at, jj in ((7, 0), (9, 1)):
            @pl.when(i == at)
            def _():
                finish(jj)

        return 0

    lax.fori_loop(0, 10, step, 0)

    for a in range(2):
        @pl.when(has_down)
        def _():
            right_copy(0, a).wait_recv()

            @pl.when(has_up)
            def _():
                right_copy(1, a).start()

        @pl.when(p + 2 < pairs)
        def _():
            left_copy(1, a).wait_recv()

            @pl.when(has_down)
            def _():
                left_copy(2, a).start()

    for j in range(2):
        attn_copy(j).wait_recv()

    per_side = CHUNKS // 2

    def first_copy(b, r):
        return copy(sum1.at[b, r], sum1.at[b, r], s1_send.at[b, r], s1_recv.at[b, r], s, near)

    def second_copy(b, r):
        return copy(sum2.at[b, r], sum2.at[b, r], s2_send.at[b, r], s2_recv.at[b, r], s, far)

    def third_copy(g, r):
        return copy(give3.at[g, r], got3.at[g, r], s3_send.at[g, r], s3_recv.at[g, r], mate, h)

    def odd(b):
        return lax.rem(b // groups + h, 2) == 1

    def block_step(e, _):
        d = (e + 1) // 2
        from_up = lax.rem(e, 2) == 1
        b = jnp.where(from_up, p + d, p - d)
        exists = (b >= 0) & (b < pairs)
        b = jnp.clip(b, 0, pairs - 1)

        @pl.when(exists & (e >= 4))
        def _():
            for a in range(2):
                @pl.when(from_up)
                def _():
                    left_copy(d - 1, a).wait_recv()

                    @pl.when(has_down)
                    def _():
                        left_copy(d, a).start()

                @pl.when(jnp.logical_not(from_up))
                def _():
                    right_copy(d - 1, a).wait_recv()

                    @pl.when(has_up)
                    def _():
                        right_copy(d, a).start()

        @pl.when(exists)
        def _():
            away = odd(b)

            def chunk(r, _):
                side = r // per_side
                at = pl.multiple_of(lax.rem(r, per_side) * part, part)
                y = (jnp.dot(both[side, 0, pl.ds(at, part), :], wbuf[b, :half, :],
                             preferred_element_type=jnp.float32)
                     + jnp.dot(both[side, 1, pl.ds(at, part), :], wbuf[b, half:, :],
                               preferred_element_type=jnp.float32))

                @pl.when(away)
                def _():
                    sum1[b, r] = y.astype(jnp.bfloat16)
                    first_copy(b, r).start()

                @pl.when(jnp.logical_not(away))
                def _():
                    tmp[r] = y

                return 0

            lax.fori_loop(0, CHUNKS, chunk, 0)

            @pl.when(jnp.logical_not(away))
            def _():
                home = b // groups == h
                g = lax.rem(b, groups)

                def settle(r, _):
                    first_copy(b, r).wait_recv()
                    y = tmp[r] + sum1[b, r].astype(jnp.float32)

                    @pl.when(home)
                    def _():
                        keep[g, r] = y

                    @pl.when(jnp.logical_not(home))
                    def _():
                        sum2[b, r] = y.astype(jnp.bfloat16)
                        second_copy(b, r).start()

                    return 0

                lax.fori_loop(0, CHUNKS, settle, 0)

        return 0

    lax.fori_loop(0, 2 * pairs - 1, block_step, 0)

    def result(g, r):
        b = h * groups + g
        second_copy(b, r).wait_recv()
        return (keep[g, r] + sum2[b, r].astype(jnp.float32)).astype(jnp.bfloat16)

    def place(g, at, member, value):
        for mm in range(2):
            @pl.when(member == mm)
            def _():
                c = (2 * g + mm) * wc
                out_ref[at:at + part, c:c + wc] = value

    for g in range(groups):
        for r in range(per_side):
            give3[g, r] = result(g, r)
            third_copy(g, r).start()
    for g in range(groups):
        for r in range(per_side, CHUNKS):
            place(g, (r - per_side) * part, m, result(g, r))
    for g in range(groups):
        for r in range(per_side):
            third_copy(g, r).wait_recv()
            place(g, r * part, 1 - m, got3[g, r])

    for j in range(2):
        @pl.when(has_next)
        def _():
            for c in kv_copies(0, 2, j, kvz_send.at[0], right):
                c.wait_send()

        @pl.when((s >= 2) & has_next)
        def _():
            for c in kv_copies(2, 4, j, kvz_send.at[1], right):
                c.wait_send()

        @pl.when(m == 0)
        def _():
            for c in kv_copies(0, 1, j, kvy_send.at[0], mate):
                c.wait_send()

        @pl.when(s >= 2)
        def _():
            for c in kv_copies(2, 3 - 2 * m, j, kvy_send.at[1], mate):
                c.wait_send()

        @pl.when((s >= 4) & (m == 1))
        def _():
            for c in kv_copies(4, 3, j, kvy_send.at[2], mate):
                c.wait_send()

        attn_copy(j).wait_send()
        for t in range(pairs - 1):
            @pl.when(has_down & (p + t < pairs))
            def _():
                left_copy(t, j).wait_send()

            @pl.when(has_up & (p - t >= 0))
            def _():
                right_copy(t, j).wait_send()

    def drain(b, _):
        for r in range(CHUNKS):
            @pl.when(odd(b))
            def _():
                first_copy(b, r).wait_send()

            @pl.when(jnp.logical_not(odd(b)) & (b // groups != h))
            def _():
                second_copy(b, r).wait_send()

        return 0

    lax.fori_loop(0, pairs, drain, 0)
    for g in range(groups):
        for r in range(per_side):
            third_copy(g, r).wait_send()


def body(n_seq, queries, keys, values, doc_lengths, out_weight):
    rows, width = queries.shape
    kv_width = keys.shape[1]
    depth, wc = out_weight.shape
    pairs = n_seq // 2
    groups = pairs // 4
    heads = width // DH
    part = rows * 2 // CHUNKS
    slots = -(-(MOST - 1) // rows) + 1
    vmem = pl.BlockSpec(memory_space=pltpu.VMEM)
    hbm = pl.BlockSpec(memory_space=pl.ANY)
    bf, f32, dma = jnp.bfloat16, jnp.float32, pltpu.SemaphoreType.DMA
    return pl.pallas_call(
        functools.partial(kernel, n_seq),
        out_shape=jax.ShapeDtypeStruct((rows, wc * 2 * (pairs // 4)), bf),
        in_specs=[pl.BlockSpec(memory_space=pltpu.SMEM), vmem, hbm, hbm, hbm],
        out_specs=vmem,
        scratch_shapes=[
            pltpu.VMEM((slots, rows, kv_width), bf),
            pltpu.VMEM((slots, rows, kv_width), bf),
            pltpu.VMEM((pairs, depth, wc), bf),
            pltpu.VMEM((rows, rows), f32),
            pltpu.VMEM((DH, rows), bf),
            pltpu.VMEM((heads, 1, rows), f32),
            pltpu.VMEM((heads, 1, rows), f32),
            pltpu.VMEM((heads, DH, rows), f32),
            pltpu.VMEM((2, 2, rows, width // 2), bf),
            pltpu.VMEM((CHUNKS, part, wc), f32),
            pltpu.VMEM((groups, CHUNKS, part, wc), f32),
            pltpu.VMEM((pairs, CHUNKS, part, wc), bf),
            pltpu.VMEM((pairs, CHUNKS, part, wc), bf),
            pltpu.VMEM((groups, CHUNKS // 2, part, wc), bf),
            pltpu.VMEM((groups, CHUNKS // 2, part, wc), bf),
            dma((3,)), dma((2, 2, 2)), dma((3, 2, 2)), dma((slots, 2, 2)),
            dma((pairs, 2)), dma((pairs, 2)), dma((pairs, 2)), dma((pairs, 2)),
            dma((2,)), dma((2,)), dma((pairs, CHUNKS)), dma((pairs, CHUNKS)),
            dma((pairs, CHUNKS)), dma((pairs, CHUNKS)),
            dma((groups, CHUNKS // 2)), dma((groups, CHUNKS // 2)),
        ],
        compiler_params=pltpu.CompilerParams(
            collective_id=0, has_side_effects=True, vmem_limit_bytes=56 * 1024 * 1024
        ),
    )(doc_lengths, queries, keys, values, out_weight)


def solution(mesh):
    return jax.shard_map(
        functools.partial(body, mesh.shape["seq"]),
        mesh=mesh,
        in_specs=(P("seq", "head"), P("seq", "head"), P("seq", "head"), P(), P("head", "seq")),
        out_specs=P("seq", "head"),
        check_vma=False,
    )
```

profile of v0, /device:TPU:24, one launch (start us, length us, event | category | flops | bytes accessed | tf_op | source)
XLA Modules:
  0.0 115.4 jit_solution(9814270080521593412)
XLA Ops:
  0.0 113.1 %shard_map.55 = bf16[512,1024]{1,0:T(8,128)(2,1)} custom-call(s32[16]{0:T(128)} %lens_ref.1, bf16[512,1024]{1,0:T(8,128)(2,1)} %q_ref.1, bf16[512,256]{1,0:T(8,128)(2,1)} %k_hbm.1, bf16[512,256]{1,0:T(8,128)(2,1)} %v_hbm.1, bf16[1024,512]{1,0:T(8,128)(2,1)} %w_hbm.1), custom_call_target="tpu_custom_call" | custom-call | tf_op jit(solution)/shard_map/pallas_call | solution.py:407
  113.1 2.3 %copy.7 = bf16[512,1024]{1,0:T(8,128)(2,1)} copy(bf16[512,1024]{1,0:T(8,128)(2,1)} %shard_map.55) | data formatting | bytes 2097152
where the time goes:
time: 116 us; the launch traced here: 115 us
  Pallas kernels  113 us (97%)
  local copies, waits for them, and re-layouts  2.26 us (2%)
    pallas_call x1, Pallas kernels, body(): pl.pallas_call(functools.partial(kernel, n_seq), out_shape=jax.ShapeDtype...  113 us

commit v1 on v0

v1 whole, which is shorter than its diff:
```python
import functools
import math

import jax
import jax.numpy as jnp
from jax import lax
from jax.experimental import pallas as pl
from jax.experimental.pallas import tpu as pltpu
from jax.sharding import PartitionSpec as P

HQ = 32
KV = 8
DH = 128
MOST = 2048
CHUNKS = 4
PIECE = 128
MESH = pl.DeviceIdType.MESH


def kernel(
    n_seq, lens_ref, q_ref, k_hbm, v_hbm, w_hbm, out_ref,
    kbuf, vbuf, wbuf, bias, vt, mx, sm, acc, both,
    tmp, keep, sum1, sum2, give3, got3,
    load_sem, kvz_send, kvy_send, kv_recv, wl_send, wl_recv, wr_send, wr_recv,
    at_send, at_recv, s1_send, s1_recv, s2_send, s2_recv, s3_send, s3_recv,
):
    s, h = lax.axis_index("seq"), lax.axis_index("head")
    pairs = n_seq // 2
    p, m = s // 2, lax.rem(s, 2)
    mate = s + 1 - 2 * m
    right = lax.rem(p + 1, pairs) * 2 + m
    left = lax.rem(p + pairs - 1, pairs) * 2 + m
    near = h + 1 - 2 * lax.rem(h, 2)
    far = lax.rem(h + 2, 4)
    rows = q_ref.shape[0]
    depth, wc = w_hbm.shape
    pieces, wcp = wbuf.shape[1], wbuf.shape[3]
    half = depth // 2
    groups = pairs // 4
    group_size = HQ // KV
    part = rows * 2 // CHUNKS
    has_up, has_down = p + 1 < pairs, p >= 1
    scale = DH ** (-0.5) * math.log2(math.e)

    def copy(src, dst, send, recv, seq, head):
        return pltpu.make_async_remote_copy(
            src_ref=src, dst_ref=dst, send_sem=send, recv_sem=recv,
            device_id={"seq": seq, "head": head}, device_id_type=MESH,
        )

    def kv_copies(src_slot, dst_slot, j, send, target):
        cols = pl.ds(pl.multiple_of(j * DH, DH), DH)
        return [
            copy(buf.at[src_slot, :, cols], buf.at[dst_slot, :, cols],
                 send.at[j, c], kv_recv.at[dst_slot, j, c], target, h)
            for c, buf in enumerate((kbuf, vbuf))
        ]

    def w_copy(block, c, step, send, recv, target):
        piece = wbuf.at[block, c]
        return copy(piece, piece, send.at[step, c], recv.at[step, c], target, h)

    def left_copy(step, c):
        return w_copy(jnp.minimum(p + step, pairs - 1), c, step, wl_send, wl_recv, left)

    def right_copy(step, c):
        return w_copy(jnp.maximum(p - step, 0), c, step, wr_send, wr_recv, right)

    loads = [
        pltpu.make_async_copy(k_hbm, kbuf.at[0], load_sem.at[0]),
        pltpu.make_async_copy(v_hbm, vbuf.at[0], load_sem.at[1]),
    ] + [
        pltpu.make_async_copy(w_hbm.at[:, c * wcp:(c + 1) * wcp], wbuf.at[p, c], load_sem.at[2 + c])
        for c in range(pieces)
    ]
    for load in loads:
        load.start()

    barrier = pltpu.get_barrier_semaphore()
    for seq, head in ((mate, h), (left, h), (right, h), (s, near), (s, far)):
        pl.semaphore_signal(barrier, inc=1, device_id={"seq": seq, "head": head}, device_id_type=MESH)
    pl.semaphore_wait(barrier, 5)

    loads[0].wait()
    loads[1].wait()
    has_next = s + 2 < n_seq
    for j in range(2):
        @pl.when(has_next)
        def _():
            for c in kv_copies(0, 2, j, kvz_send.at[0], right):
                c.start()

        @pl.when(m == 0)
        def _():
            for c in kv_copies(0, 1, j, kvy_send.at[0], mate):
                c.start()

    for load in loads[2:]:
        load.wait()

    @pl.when(has_down)
    def _():
        for c in range(pieces):
            left_copy(0, c).start()

    q_pos = s * rows + lax.broadcasted_iota(jnp.int32, (1, rows), 1)
    start = jnp.int32(0)
    first = jnp.zeros((1, rows), jnp.int32)
    for d in range(1, lens_ref.shape[0]):
        start = start + lens_ref[d - 1]
        first = jnp.where(q_pos >= start, start, first)

    def attn_copy(j):
        return copy(both.at[1, j], both.at[0, j], at_send.at[j], at_recv.at[j], mate, h)

    def finish(j):
        def one(g, _):
            i = j * group_size + g
            full = jnp.transpose(acc[i] / sm[i])
            both[1, j, :, pl.ds(pl.multiple_of(g * DH, DH), DH)] = full.astype(jnp.bfloat16)
            return 0

        lax.fori_loop(0, group_size, one, 0)
        attn_copy(j).start()

    def take_left(t, c):
        left_copy(t, c).wait_recv()

        @pl.when(has_down)
        def _():
            left_copy(t + 1, c).start()

    def take_right(t, c):
        right_copy(t, c).wait_recv()

        @pl.when(has_up)
        def _():
            right_copy(t + 1, c).start()

    def step(i, _):
        k = jnp.maximum(i - 2, 0)
        w = lax.rem(k, 4)
        slot = jnp.where(i < 2, 0, 2 + 2 * (k // 4) - lax.rem(w, 2))
        j = jnp.where(i < 2, i, w // 2)

        @pl.when((i >= 2) & (s >= slot))
        def _():
            for c in kv_copies(slot, slot, j, kvz_send.at[0], right):
                c.wait_recv()

            @pl.when((slot == 2) & has_next)
            def _():
                for c in kv_copies(2, 4, j, kvz_send.at[1], right):
                    c.start()

            @pl.when(slot == 2)
            def _():
                for c in kv_copies(2, 3 - 2 * m, j, kvy_send.at[1], mate):
                    c.start()

            @pl.when((slot == 4) & (m == 1))
            def _():
                for c in kv_copies(4, 3, j, kvy_send.at[2], mate):
                    c.start()

        @pl.when((i == 4) & has_up)
        def _():
            for c in range(pieces):
                right_copy(0, c).start()

        for c in range(pieces):
            @pl.when((i == 11 - 2 * (pieces - c)) & has_up)
            def _():
                take_left(0, c)

        @pl.when(s >= slot)
        def _():
            cols = pl.ds(pl.multiple_of(j * DH, DH), DH)
            k_pos = (s - slot) * rows + lax.broadcasted_iota(jnp.int32, (rows, rows), 0)
            bias[...] = jnp.where((k_pos >= first) & (k_pos <= q_pos), 0.0, -1e30)
            vt[...] = jnp.transpose(vbuf[slot, :, cols])

            def one(g, _):
                at = j * group_size + g
                q = q_ref[:, pl.ds(pl.multiple_of(at * DH, DH), DH)]
                scores = lax.dot_general(
                    kbuf[slot, :, cols], q, (((1,), (1,)), ((), ())),
                    preferred_element_type=jnp.float32,
                ) * scale + bias[...]
                top = jnp.max(scores, axis=0, keepdims=True)
                old = jnp.where(i < 2, jnp.full_like(top, -1e30), mx[at])
                new = jnp.maximum(old, top)
                probs = jnp.exp2(scores - new)
                fade = jnp.exp2(old - new)
                mx[at] = new
                total = jnp.sum(probs, axis=0, keepdims=True)
                sm[at] = jnp.where(i < 2, total, sm[at] * fade + total)
                mixed = jnp.dot(vt[...], probs.astype(jnp.bfloat16), preferred_element_type=jnp.float32)

                @pl.when(i < 2)
                def _():
                    acc[at] = mixed

                @pl.when(i >= 2)
                def _():
                    acc[at] = acc[at] * fade + mixed

                return 0

            lax.fori_loop(0, group_size, one, 0)

        for at, jj in ((7, 0), (9, 1)):
            @pl.when(i == at)
            def _():
                finish(jj)

        return 0

    lax.fori_loop(0, 10, step, 0)

    for j in range(2):
        attn_copy(j).wait_recv()

    per_side = CHUNKS // 2

    def first_copy(b, c, r):
        return copy(sum1.at[b, c, r], sum1.at[b, c, r], s1_send.at[b, c, r], s1_recv.at[b, c, r], s, near)

    def second_copy(b, c, r):
        return copy(sum2.at[b, c, r], sum2.at[b, c, r], s2_send.at[b, c, r], s2_recv.at[b, c, r], s, far)

    def third_copy(g, c, r):
        return copy(give3.at[g, c, r], got3.at[g, c, r], s3_send.at[g, c, r], s3_recv.at[g, c, r], mate, h)

    def odd(b):
        return lax.rem(b // groups + h, 2) == 1

    def piece_step(b, c):
        away = odd(b)

        def chunk(r, _):
            side = r // per_side
            at = pl.multiple_of(lax.rem(r, per_side) * part, part)
            y = (jnp.dot(both[side, 0, pl.ds(at, part), :], wbuf[b, c, :half, :],
                         preferred_element_type=jnp.float32)
                 + jnp.dot(both[side, 1, pl.ds(at, part), :], wbuf[b, c, half:, :],
                           preferred_element_type=jnp.float32))

            @pl.when(away)
            def _():
                sum1[b, c, r] = y.astype(jnp.bfloat16)
                first_copy(b, c, r).start()

            @pl.when(jnp.logical_not(away))
            def _():
                tmp[r] = y

            return 0

        lax.fori_loop(0, CHUNKS, chunk, 0)

        @pl.when(jnp.logical_not(away))
        def _():
            home = b // groups == h
            g = lax.rem(b, groups)

            def settle(r, _):
                first_copy(b, c, r).wait_recv()
                y = tmp[r] + sum1[b, c, r].astype(jnp.float32)

                @pl.when(home)
                def _():
                    keep[g, c, r] = y

                @pl.when(jnp.logical_not(home))
                def _():
                    sum2[b, c, r] = y.astype(jnp.bfloat16)
                    second_copy(b, c, r).start()

                return 0

            lax.fori_loop(0, CHUNKS, settle, 0)

    def block_step(e, _):
        d = (e + 1) // 2
        from_up = lax.rem(e, 2) == 1
        b = jnp.where(from_up, p + d, p - d)
        exists = (b >= 0) & (b < pairs)
        b = jnp.clip(b, 0, pairs - 1)

        @pl.when(exists)
        def _():
            def one(c, _):
                @pl.when((e >= 4) & from_up)
                def _():
                    take_left(d - 1, c)

                @pl.when((e >= 4) & jnp.logical_not(from_up))
                def _():
                    take_right(d - 1, c)

                piece_step(b, c)
                return 0

            lax.fori_loop(0, pieces, one, 0)

        @pl.when((e == 0) & has_down)
        def _():
            for c in range(pieces):
                take_right(0, c)

        @pl.when((e == 1) & (p + 2 < pairs))
        def _():
            for c in range(pieces):
                take_left(1, c)

        return 0

    lax.fori_loop(0, 2 * pairs - 1, block_step, 0)

    def result(g, c, r):
        b = h * groups + g
        second_copy(b, c, r).wait_recv()
        return (keep[g, c, r] + sum2[b, c, r].astype(jnp.float32)).astype(jnp.bfloat16)

    def place(g, c, r, member, value):
        at = pl.multiple_of(lax.rem(r, per_side) * part, part)
        first_col = pl.multiple_of((2 * g + member) * wc + c * wcp, wcp)
        out_ref[pl.ds(at, part), pl.ds(first_col, wcp)] = value

    for g in range(groups):
        def pass_on(c, _):
            for r in range(per_side):
                give3[g, c, r] = result(g, c, r)
                third_copy(g, c, r).start()
            for r in range(per_side, CHUNKS):
                place(g, c, r, m, result(g, c, r))
            return 0

        lax.fori_loop(0, pieces, pass_on, 0)

    for g in range(groups):
        def take_in(c, _):
            for r in range(per_side):
                third_copy(g, c, r).wait_recv()
                place(g, c, r, 1 - m, got3[g, c, r])
            return 0

        lax.fori_loop(0, pieces, take_in, 0)

    for j in range(2):
        @pl.when(has_next)
        def _():
            for c in kv_copies(0, 2, j, kvz_send.at[0], right):
                c.wait_send()

        @pl.when((s >= 2) & has_next)
        def _():
            for c in kv_copies(2, 4, j, kvz_send.at[1], right):
                c.wait_send()

        @pl.when(m == 0)
        def _():
            for c in kv_copies(0, 1, j, kvy_send.at[0], mate):
                c.wait_send()

        @pl.when(s >= 2)
        def _():
            for c in kv_copies(2, 3 - 2 * m, j, kvy_send.at[1], mate):
                c.wait_send()

        @pl.when((s >= 4) & (m == 1))
        def _():
            for c in kv_copies(4, 3, j, kvy_send.at[2], mate):
                c.wait_send()

        attn_copy(j).wait_send()

    def drain(b, _):
        def one(c, _):
            @pl.when(has_down & (p + b < pairs))
            def _():
                left_copy(b, c).wait_send()

            @pl.when(has_up & (p - b >= 0))
            def _():
                right_copy(b, c).wait_send()

            for r in range(CHUNKS):
                @pl.when(odd(b))
                def _():
                    first_copy(b, c, r).wait_send()

                @pl.when(jnp.logical_not(odd(b)) & (b // groups != h))
                def _():
                    second_copy(b, c, r).wait_send()

            return 0

        return lax.fori_loop(0, pieces, one, 0)

    lax.fori_loop(0, pairs, drain, 0)
    for g in range(groups):
        def sent(c, _):
            for r in range(per_side):
                third_copy(g, c, r).wait_send()
            return 0

        lax.fori_loop(0, pieces, sent, 0)


def body(n_seq, queries, keys, values, doc_lengths, out_weight):
    rows, width = queries.shape
    kv_width = keys.shape[1]
    depth, wc = out_weight.shape
    pairs = n_seq // 2
    groups = pairs // 4
    heads = width // DH
    part = rows * 2 // CHUNKS
    wcp = min(PIECE, wc)
    pieces = wc // wcp
    slots = -(-(MOST - 1) // rows) + 1
    vmem = pl.BlockSpec(memory_space=pltpu.VMEM)
    hbm = pl.BlockSpec(memory_space=pl.ANY)
    bf, f32, dma = jnp.bfloat16, jnp.float32, pltpu.SemaphoreType.DMA
    return pl.pallas_call(
        functools.partial(kernel, n_seq),
        out_shape=jax.ShapeDtypeStruct((rows, wc * 2 * (pairs // 4)), bf),
        in_specs=[pl.BlockSpec(memory_space=pltpu.SMEM), vmem, hbm, hbm, hbm],
        out_specs=vmem,
        scratch_shapes=[
            pltpu.VMEM((slots, rows, kv_width), bf),
            pltpu.VMEM((slots, rows, kv_width), bf),
            pltpu.VMEM((pairs, pieces, depth, wcp), bf),
            pltpu.VMEM((rows, rows), f32),
            pltpu.VMEM((DH, rows), bf),
            pltpu.VMEM((heads, 1, rows), f32),
            pltpu.VMEM((heads, 1, rows), f32),
            pltpu.VMEM((heads, DH, rows), f32),
            pltpu.VMEM((2, 2, rows, width // 2), bf),
            pltpu.VMEM((CHUNKS, part, wcp), f32),
            pltpu.VMEM((groups, pieces, CHUNKS, part, wcp), f32),
            pltpu.VMEM((pairs, pieces, CHUNKS, part, wcp), bf),
            pltpu.VMEM((pairs, pieces, CHUNKS, part, wcp), bf),
            pltpu.VMEM((groups, pieces, CHUNKS // 2, part, wcp), bf),
            pltpu.VMEM((groups, pieces, CHUNKS // 2, part, wcp), bf),
            dma((2 + pieces,)), dma((2, 2, 2)), dma((3, 2, 2)), dma((slots, 2, 2)),
            dma((pairs, pieces)), dma((pairs, pieces)), dma((pairs, pieces)), dma((pairs, pieces)),
            dma((2,)), dma((2,)),
            dma((pairs, pieces, CHUNKS)), dma((pairs, pieces, CHUNKS)),
            dma((pairs, pieces, CHUNKS)), dma((pairs, pieces, CHUNKS)),
            dma((groups, pieces, CHUNKS // 2)), dma((groups, pieces, CHUNKS // 2)),
        ],
        compiler_params=pltpu.CompilerParams(
            collective_id=0, has_side_effects=True, vmem_limit_bytes=56 * 1024 * 1024
        ),
    )(doc_lengths, queries, keys, values, out_weight)


def solution(mesh):
    return jax.shard_map(
        functools.partial(body, mesh.shape["seq"]),
        mesh=mesh,
        in_specs=(P("seq", "head"), P("seq", "head"), P("seq", "head"), P(), P("head", "seq")),
        out_specs=P("seq", "head"),
        check_vma=False,
    )
```

time: 116 us -> 124 us (1.069)
  Pallas kernels: 113 us -> 121 us
    pallas_call x1, Pallas kernels: 113 us -> 121 us  [body(): pl.pallas_call(functools.partial(kernel, n_seq), out_shape=jax.ShapeDtype...]
where the time goes in v1:
time: 124 us
  Pallas kernels  121 us (98%)
  local copies, waits for them, and re-layouts  2.26 us (2%)
    pallas_call x1, Pallas kernels, body(): pl.pallas_call(functools.partial(kernel, n_seq), out_shape=jax.ShapeDtype...  121 us

profile of v1, /device:TPU:24, one launch (start us, length us, event | category | flops | bytes accessed | tf_op | source)
XLA Modules:
  0.0 123.6 jit_solution(11059378405324553603)
XLA Ops:
  0.0 121.3 %shard_map.55 = bf16[512,1024]{1,0:T(8,128)(2,1)} custom-call(s32[16]{0:T(128)} %lens_ref.1, bf16[512,1024]{1,0:T(8,128)(2,1)} %q_ref.1, bf16[512,256]{1,0:T(8,128)(2,1)} %k_hbm.1, bf16[512,256]{1,0:T(8,128)(2,1)} %v_hbm.1, bf16[1024,512]{1,0:T(8,128)(2,1)} %w_hbm.1), custom_call_target="tpu_custom_call" | custom-call | tf_op jit(solution)/shard_map/pallas_call | solution.py:426
  121.3 2.3 %copy.7 = bf16[512,1024]{1,0:T(8,128)(2,1)} copy(bf16[512,1024]{1,0:T(8,128)(2,1)} %shard_map.55) | data formatting | bytes 2097152

commit v2 on v1

--- a/solution.py
+++ b/solution.py
@@ -20,9 +20,10 @@
 def kernel(
     n_seq, lens_ref, q_ref, k_hbm, v_hbm, w_hbm, out_ref,
     kbuf, vbuf, wbuf, bias, vt, mx, sm, acc, both,
-    tmp, keep, sum1, sum2, give3, got3,
+    tmp, keep, sum1, sum2, give3, got3, lent, lsum1, lsum2, lgot,
     load_sem, kvz_send, kvy_send, kv_recv, wl_send, wl_recv, wr_send, wr_recv,
     at_send, at_recv, s1_send, s1_recv, s2_send, s2_recv, s3_send, s3_recv,
+    la_send, la_recv, l1_send, l1_recv, l2_send, l2_recv,
 ):
     s, h = lax.axis_index("seq"), lax.axis_index("head")
     pairs = n_seq // 2
@@ -39,7 +40,9 @@
     groups = pairs // 4
     group_size = HQ // KV
     part = rows * 2 // CHUNKS
+    wide = 2 if pieces % 2 == 0 else 1
     has_up, has_down = p + 1 < pairs, p >= 1
+    is_last, is_helper = p == pairs - 1, p == pairs - 2
     scale = DH ** (-0.5) * math.log2(math.e)
 
     def copy(src, dst, send, recv, seq, head):
@@ -113,6 +116,12 @@
     def attn_copy(j):
         return copy(both.at[1, j], both.at[0, j], at_send.at[j], at_recv.at[j], mate, h)
 
+    def lend_own(j):
+        return copy(both.at[1, j], lent.at[1, j], la_send.at[0, j], la_recv.at[0, j], left, h)
+
+    def lend_other(j, source, target):
+        return copy(source, lent.at[0, j], la_send.at[1, j], la_recv.at[1, j], target, h)
+
     def finish(j):
         def one(g, _):
             i = j * group_size + g
@@ -123,6 +132,10 @@
         lax.fori_loop(0, group_size, one, 0)
         attn_copy(j).start()
 
+        @pl.when(is_last)
+        def _():
+            lend_own(j).start()
+
     def take_left(t, c):
         left_copy(t, c).wait_recv()
 
@@ -133,7 +146,7 @@
     def take_right(t, c):
         right_copy(t, c).wait_recv()
 
-        @pl.when(has_up)
+        @pl.when(has_up & jnp.logical_not(is_helper & (p == t + 1)))
         def _():
             right_copy(t + 1, c).start()
 
@@ -209,7 +222,7 @@
 
             lax.fori_loop(0, group_size, one, 0)
 
-        for at, jj in ((7, 0), (9, 1)):
+        for at, jj in ((8, 0), (9, 1)):
             @pl.when(i == at)
             def _():
                 finish(jj)
@@ -217,9 +230,6 @@
         return 0
 
     lax.fori_loop(0, 10, step, 0)
-
-    for j in range(2):
-        attn_copy(j).wait_recv()
 
     per_side = CHUNKS // 2
 
@@ -235,38 +245,46 @@
     def odd(b):
         return lax.rem(b // groups + h, 2) == 1
 
-    def piece_step(b, c):
-        away = odd(b)
-
-        def chunk(r, _):
-            side = r // per_side
-            at = pl.multiple_of(lax.rem(r, per_side) * part, part)
-            y = (jnp.dot(both[side, 0, pl.ds(at, part), :], wbuf[b, c, :half, :],
-                         preferred_element_type=jnp.float32)
-                 + jnp.dot(both[side, 1, pl.ds(at, part), :], wbuf[b, c, half:, :],
-                           preferred_element_type=jnp.float32))
-
-            @pl.when(away)
-            def _():
-                sum1[b, c, r] = y.astype(jnp.bfloat16)
-                first_copy(b, c, r).start()
-
-            @pl.when(jnp.logical_not(away))
-            def _():
-                tmp[r] = y
-
-            return 0
-
-        lax.fori_loop(0, CHUNKS, chunk, 0)
-
-        @pl.when(jnp.logical_not(away))
+    def product(source, b, c, n, r):
+        side = r // per_side
+        at = pl.multiple_of(lax.rem(r, per_side) * part, part)
+
+        def weights(lo):
+            return jnp.concatenate([wbuf[b, c + i, lo:lo + half, :] for i in range(n)], axis=1)
+
+        y = (jnp.dot(source[side, 0, pl.ds(at, part), :], weights(0), preferred_element_type=jnp.float32)
+             + jnp.dot(source[side, 1, pl.ds(at, part), :], weights(half), preferred_element_type=jnp.float32))
+        return [y[:, i * wcp:(i + 1) * wcp] for i in range(n)]
+
+    def compute(b, c, n, lo, hi):
+        @pl.when(odd(b))
+        def _():
+            def chunk(r, _):
+                for i, y in enumerate(product(both, b, c, n, r)):
+                    sum1[b, c + i, r] = y.astype(jnp.bfloat16)
+                    first_copy(b, c + i, r).start()
+                return 0
+
+            lax.fori_loop(lo, hi, chunk, 0, unroll=True)
+
+        @pl.when(jnp.logical_not(odd(b)))
+        def _():
+            def chunk(r, _):
+                for i, y in enumerate(product(both, b, c, n, r)):
+                    tmp[c + i, r] = y
+                return 0
+
+            lax.fori_loop(lo, hi, chunk, 0, unroll=True)
+
+    def settle(b, c, lo, hi):
+        @pl.when(jnp.logical_not(odd(b)))
         def _():
             home = b // groups == h
             g = lax.rem(b, groups)
 
-            def settle(r, _):
+            def one(r, _):
                 first_copy(b, c, r).wait_recv()
-                y = tmp[r] + sum1[b, c, r].astype(jnp.float32)
+                y = tmp[c, r] + sum1[b, c, r].astype(jnp.float32)
 
                 @pl.when(home)
                 def _():
@@ -279,44 +297,191 @@
 
                 return 0
 
-            lax.fori_loop(0, CHUNKS, settle, 0)
-
-    def block_step(e, _):
+            lax.fori_loop(lo, hi, one, 0)
+
+    def block_side(b, side):
+        lo, hi = side * per_side, (side + 1) * per_side
+
+        def first(k, _):
+            compute(b, k * wide, wide, lo, hi)
+            return 0
+
+        def second(c, _):
+            settle(b, c, lo, hi)
+            return 0
+
+        lax.fori_loop(0, pieces // wide, first, 0)
+        lax.fori_loop(0, pieces, second, 0)
+
+    def lent_first(c, r):
+        return copy(lsum1.at[c, r], lsum1.at[c, r], l1_send.at[c, r], l1_recv.at[c, r], s, near)
+
+    def lent_result(c, r):
+        return copy(lsum2.at[c, r], lgot.at[c, r], l2_send.at[c, r], l2_recv.at[c, r], right, h)
+
+    def lent_second(c, r):
+        return copy(lgot.at[c, r], sum2.at[0, c, r], s2_send.at[0, c, r], s2_recv.at[0, c, r], s, far)
+
+    def help_step(c, side):
+        at = side * per_side
+
+        @pl.when(odd(0))
+        def _():
+            def chunk(r, _):
+                lsum1[c, r] = product(lent, 0, c, 1, r)[0].astype(jnp.bfloat16)
+                lent_first(c, r).start()
+                return 0
+
+            lax.fori_loop(at, at + per_side, chunk, 0, unroll=True)
+
+        @pl.when(jnp.logical_not(odd(0)))
+        def _():
+            def chunk(r, _):
+                tmp[c, r] = product(lent, 0, c, 1, r)[0]
+                return 0
+
+            lax.fori_loop(at, at + per_side, chunk, 0, unroll=True)
+
+            def settle(r, _):
+                lent_first(c, r).wait_recv()
+                lsum2[c, r] = (tmp[c, r] + lsum1[c, r].astype(jnp.float32)).astype(jnp.bfloat16)
+                lent_result(c, r).start()
+                return 0
+
+            lax.fori_loop(at, at + per_side, settle, 0)
+
+    def in_order(one):
+        def early(side):
+            def each(c, _):
+                one(c, side)
+                return 0
+
+            lax.fori_loop(0, pieces - 1, each, 0)
+
+        early(1)
+        early(0)
+        for side in range(2):
+            one(pieces - 1, side)
+
+    def take_lent(c, side):
+        @pl.when(jnp.logical_not(odd(0)))
+        def _():
+            def each(r, _):
+                lent_result(c, r).wait_recv()
+
+                @pl.when(h == 0)
+                def _():
+                    keep[0, c, r] = lgot[c, r].astype(jnp.float32)
+
+                @pl.when(h != 0)
+                def _():
+                    lent_second(c, r).start()
+
+                return 0
+
+            lax.fori_loop(side * per_side, (side + 1) * per_side, each, 0)
+
+    def block_at(e):
         d = (e + 1) // 2
         from_up = lax.rem(e, 2) == 1
         b = jnp.where(from_up, p + d, p - d)
-        exists = (b >= 0) & (b < pairs)
-        b = jnp.clip(b, 0, pairs - 1)
+        return jnp.clip(b, 0, pairs - 1), (b >= 0) & (b < pairs), from_up, d
+
+    def take_early(c):
+        @pl.when(has_down)
+        def _():
+            take_right(0, c)
+
+        @pl.when(p + 2 < pairs)
+        def _():
+            take_left(1, c)
+
+    def own_side(e, _):
+        for c in range(pieces):
+            @pl.when(e == (c if c < min(pieces - 1, 2) else 2))
+            def _():
+                take_early(c)
+
+        b, exists, _, _ = block_at(e)
 
         @pl.when(exists)
         def _():
+            block_side(b, 1)
+
+        return 0
+
+    lax.fori_loop(0, 4, own_side, 0)
+
+    for j in range(2):
+        attn_copy(j).wait_recv()
+        if j == 0:
+            @pl.when(is_last)
+            def _():
+                lend_other(0, both.at[0, 0], left).start()
+
+    def other_side(e, _):
+        b, exists, _, _ = block_at(e)
+
+        @pl.when(exists)
+        def _():
+            block_side(b, 0)
+
+        @pl.when(is_helper & (e == 0))
+        def _():
+            for j in range(2):
+                lend_own(j).wait_recv()
+            lend_other(1, lent.at[1, 1], mate).start()
+
+        return 0
+
+    lax.fori_loop(0, 4, other_side, 0)
+
+    def block_step(e, _):
+        b, exists, from_up, d = block_at(e)
+        helped = is_last & (b == 0)
+        helping = is_helper & (b == 0)
+
+        @pl.when(exists & jnp.logical_not(helped))
+        def _():
             def one(c, _):
-                @pl.when((e >= 4) & from_up)
+                @pl.when(from_up)
                 def _():
                     take_left(d - 1, c)
 
-                @pl.when((e >= 4) & jnp.logical_not(from_up))
+                @pl.when(jnp.logical_not(from_up))
                 def _():
                     take_right(d - 1, c)
 
-                piece_step(b, c)
+                @pl.when(helping & (c == pieces - 1))
+                def _():
+                    for j in range(2):
+                        lend_other(j, both.at[0, 0], left).wait_recv()
+
+                    def other(k, _):
+                        help_step(k, 0)
+                        return 0
+
+                    lax.fori_loop(0, pieces, other, 0)
+                    help_step(c, 1)
+
+                compute(b, c, 1, 0, CHUNKS)
+                settle(b, c, 0, CHUNKS)
+
+                @pl.when(helping & (c < pieces - 1))
+                def _():
+                    help_step(c, 1)
+
                 return 0
 
             lax.fori_loop(0, pieces, one, 0)
 
-        @pl.when((e == 0) & has_down)
-        def _():
-            for c in range(pieces):
-                take_right(0, c)
-
-        @pl.when((e == 1) & (p + 2 < pairs))
-        def _():
-            for c in range(pieces):
-                take_left(1, c)
+        @pl.when(helped)
+        def _():
+            in_order(take_lent)
 
         return 0
 
-    lax.fori_loop(0, 2 * pairs - 1, block_step, 0)
+    lax.fori_loop(4, 2 * pairs - 1, block_step, 0)
 
     def result(g, c, r):
         b = h * groups + g
@@ -329,15 +494,16 @@
         out_ref[pl.ds(at, part), pl.ds(first_col, wcp)] = value
 
     for g in range(groups):
-        def pass_on(c, _):
-            for r in range(per_side):
-                give3[g, c, r] = result(g, c, r)
-                third_copy(g, c, r).start()
-            for r in range(per_side, CHUNKS):
-                place(g, c, r, m, result(g, c, r))
-            return 0
-
-        lax.fori_loop(0, pieces, pass_on, 0)
+        def pass_on(c, side):
+            for r in range(side * per_side, (side + 1) * per_side):
+                value = result(g, c, r)
+                if side:
+                    place(g, c, r, m, value)
+                else:
+                    give3[g, c, r] = value
+                    third_copy(g, c, r).start()
+
+        in_order(pass_on)
 
     for g in range(groups):
         def take_in(c, _):
@@ -382,12 +548,12 @@
             def _():
                 left_copy(b, c).wait_send()
 
-            @pl.when(has_up & (p - b >= 0))
+            @pl.when(has_up & (p - b >= 0) & jnp.logical_not(is_helper & (p == b)))
             def _():
                 right_copy(b, c).wait_send()
 
             for r in range(CHUNKS):
-                @pl.when(odd(b))
+                @pl.when(odd(b) & jnp.logical_not(is_last & (b == 0)))
                 def _():
                     first_copy(b, c, r).wait_send()
 
@@ -400,6 +566,31 @@
         return lax.fori_loop(0, pieces, one, 0)
 
     lax.fori_loop(0, pairs, drain, 0)
+
+    @pl.when(is_last)
+    def _():
+        for j in range(2):
+            lend_own(j).wait_send()
+        lend_other(0, both.at[0, 0], left).wait_send()
+
+    @pl.when(is_helper)
+    def _():
+        lend_other(1, lent.at[1, 1], mate).wait_send()
+
+        def one(c, _):
+            for r in range(CHUNKS):
+                @pl.when(odd(0))
+                def _():
+                    lent_first(c, r).wait_send()
+
+                @pl.when(jnp.logical_not(odd(0)))
+                def _():
+                    lent_result(c, r).wait_send()
+
+            return 0
+
+        lax.fori_loop(0, pieces, one, 0)
+
     for g in range(groups):
         def sent(c, _):
             for r in range(per_side):
@@ -438,18 +629,24 @@
             pltpu.VMEM((heads, 1, rows), f32),
             pltpu.VMEM((heads, DH, rows), f32),
             pltpu.VMEM((2, 2, rows, width // 2), bf),
-            pltpu.VMEM((CHUNKS, part, wcp), f32),
+            pltpu.VMEM((pieces, CHUNKS, part, wcp), f32),
             pltpu.VMEM((groups, pieces, CHUNKS, part, wcp), f32),
             pltpu.VMEM((pairs, pieces, CHUNKS, part, wcp), bf),
             pltpu.VMEM((pairs, pieces, CHUNKS, part, wcp), bf),
             pltpu.VMEM((groups, pieces, CHUNKS // 2, part, wcp), bf),
             pltpu.VMEM((groups, pieces, CHUNKS // 2, part, wcp), bf),
+            pltpu.VMEM((2, 2, rows, width // 2), bf),
+            pltpu.VMEM((pieces, CHUNKS, part, wcp), bf),
+            pltpu.VMEM((pieces, CHUNKS, part, wcp), bf),
+            pltpu.VMEM((pieces, CHUNKS, part, wcp), bf),
             dma((2 + pieces,)), dma((2, 2, 2)), dma((3, 2, 2)), dma((slots, 2, 2)),
             dma((pairs, pieces)), dma((pairs, pieces)), dma((pairs, pieces)), dma((pairs, pieces)),
             dma((2,)), dma((2,)),
             dma((pairs, pieces, CHUNKS)), dma((pairs, pieces, CHUNKS)),
             dma((pairs, pieces, CHUNKS)), dma((pairs, pieces, CHUNKS)),
             dma((groups, pieces, CHUNKS // 2)), dma((groups, pieces, CHUNKS // 2)),
+            dma((2, 2)), dma((2, 2)), dma((pieces, CHUNKS)), dma((pieces, CHUNKS)),
+            dma((pieces, CHUNKS)), dma((pieces, CHUNKS)),
         ],
         compiler_params=pltpu.CompilerParams(
             collective_id=0, has_side_effects=True, vmem_limit_bytes=56 * 1024 * 1024

time: 124 us -> 99.5 us (0.80)
  Pallas kernels: 121 us -> 97.1 us
    pallas_call x1, Pallas kernels: 121 us -> 97.1 us  [body(): pl.pallas_call(functools.partial(kernel, n_seq), out_shape=jax.ShapeDtype...]
where the time goes in v2:
time: 99.5 us; the launch traced here: 99.4 us
  Pallas kernels  97.1 us (98%)
  local copies, waits for them, and re-layouts  2.26 us (2%)
    pallas_call x1, Pallas kernels, body(): pl.pallas_call(functools.partial(kernel, n_seq), out_shape=jax.ShapeDtype...  97.1 us
    unnamed x1, local copies, waits for them, and re-layouts  2.26 us

profile of v2, /device:TPU:24, one launch (start us, length us, event | category | flops | bytes accessed | tf_op | source)
XLA Modules:
  0.0 99.4 jit_solution(1404085659129054325)
XLA Ops:
  0.0 97.1 %shard_map.55 = bf16[512,1024]{1,0:T(8,128)(2,1)} custom-call(s32[16]{0:T(128)} %lens_ref.1, bf16[512,1024]{1,0:T(8,128)(2,1)} %q_ref.1, bf16[512,256]{1,0:T(8,128)(2,1)} %k_hbm.1, bf16[512,256]{1,0:T(8,128)(2,1)} %v_hbm.1, bf16[1024,512]{1,0:T(8,128)(2,1)} %w_hbm.1), custom_call_target="tpu_custom_call" | custom-call | tf_op jit(solution)/shard_map/pallas_call | solution.py:617
  97.1 2.3 %copy.7 = bf16[512,1024]{1,0:T(8,128)(2,1)} copy(bf16[512,1024]{1,0:T(8,128)(2,1)} %shard_map.55) | data formatting | bytes 2097152

commit v3 on v2

--- a/solution.py
+++ b/solution.py
@@ -18,10 +18,10 @@
 
 
 def kernel(
-    n_seq, lens_ref, q_ref, k_hbm, v_hbm, w_hbm, out_ref,
-    kbuf, vbuf, wbuf, bias, vt, mx, sm, acc, both,
+    n_seq, lens_ref, q_hbm, k_hbm, v_hbm, w_hbm, out_hbm,
+    q_ref, out_ref, kbuf, vbuf, wbuf, bias, vt, mx, sm, acc, both,
     tmp, keep, sum1, sum2, give3, got3, lent, lsum1, lsum2, lgot,
-    load_sem, kvz_send, kvy_send, kv_recv, wl_send, wl_recv, wr_send, wr_recv,
+    load_sem, out_sem, kvz_send, kvy_send, kv_recv, wl_send, wl_recv, wr_send, wr_recv,
     at_send, at_recv, s1_send, s1_recv, s2_send, s2_recv, s3_send, s3_recv,
     la_send, la_recv, l1_send, l1_recv, l2_send, l2_recv,
 ):
@@ -61,7 +61,7 @@
 
     def w_copy(block, c, step, send, recv, target):
         piece = wbuf.at[block, c]
-        return copy(piece, piece, send.at[step, c], recv.at[step, c], target, h)
+        return copy(piece, piece, send.at[step], recv.at[step, c], target, h)
 
     def left_copy(step, c):
         return w_copy(jnp.minimum(p + step, pairs - 1), c, step, wl_send, wl_recv, left)
@@ -73,9 +73,9 @@
         pltpu.make_async_copy(k_hbm, kbuf.at[0], load_sem.at[0]),
         pltpu.make_async_copy(v_hbm, vbuf.at[0], load_sem.at[1]),
     ] + [
-        pltpu.make_async_copy(w_hbm.at[:, c * wcp:(c + 1) * wcp], wbuf.at[p, c], load_sem.at[2 + c])
+        pltpu.make_async_copy(w_hbm.at[:, c * wcp:(c + 1) * wcp], wbuf.at[p, c], load_sem.at[3 + c])
         for c in range(pieces)
-    ]
+    ] + [pltpu.make_async_copy(q_hbm, q_ref, load_sem.at[2])]
     for load in loads:
         load.start()
 
@@ -98,7 +98,7 @@
             for c in kv_copies(0, 1, j, kvy_send.at[0], mate):
                 c.start()
 
-    for load in loads[2:]:
+    for load in loads[2:-1]:
         load.wait()
 
     @pl.when(has_down)
@@ -113,6 +113,8 @@
         start = start + lens_ref[d - 1]
         first = jnp.where(q_pos >= start, start, first)
 
+    loads[-1].wait()
+
     def attn_copy(j):
         return copy(both.at[1, j], both.at[0, j], at_send.at[j], at_recv.at[j], mate, h)
 
@@ -130,8 +132,6 @@
             return 0
 
         lax.fori_loop(0, group_size, one, 0)
-        attn_copy(j).start()
-
         @pl.when(is_last)
         def _():
             lend_own(j).start()
@@ -175,6 +175,10 @@
             def _():
                 for c in kv_copies(4, 3, j, kvy_send.at[2], mate):
                     c.start()
+
+        @pl.when(i == 8)
+        def _():
+            attn_copy(0).start()
 
         @pl.when((i == 4) & has_up)
         def _():
@@ -222,7 +226,7 @@
 
             lax.fori_loop(0, group_size, one, 0)
 
-        for at, jj in ((8, 0), (9, 1)):
+        for at, jj in ((7, 0), (9, 1)):
             @pl.when(i == at)
             def _():
                 finish(jj)
@@ -230,17 +234,18 @@
         return 0
 
     lax.fori_loop(0, 10, step, 0)
+    attn_copy(1).start()
 
     per_side = CHUNKS // 2
 
     def first_copy(b, c, r):
-        return copy(sum1.at[b, c, r], sum1.at[b, c, r], s1_send.at[b, c, r], s1_recv.at[b, c, r], s, near)
+        return copy(sum1.at[b, c, r], sum1.at[b, c, r], s1_send.at[b], s1_recv.at[b, c, r], s, near)
 
     def second_copy(b, c, r):
-        return copy(sum2.at[b, c, r], sum2.at[b, c, r], s2_send.at[b, c, r], s2_recv.at[b, c, r], s, far)
+        return copy(sum2.at[b, c, r], sum2.at[b, c, r], s2_send.at[b], s2_recv.at[b, c, r], s, far)
 
     def third_copy(g, c, r):
-        return copy(give3.at[g, c, r], got3.at[g, c, r], s3_send.at[g, c, r], s3_recv.at[g, c, r], mate, h)
+        return copy(give3.at[g, c, r], got3.at[g, c, r], s3_send.at[g], s3_recv.at[g, c, r], mate, h)
 
     def odd(b):
         return lax.rem(b // groups + h, 2) == 1
@@ -256,27 +261,29 @@
              + jnp.dot(source[side, 1, pl.ds(at, part), :], weights(half), preferred_element_type=jnp.float32))
         return [y[:, i * wcp:(i + 1) * wcp] for i in range(n)]
 
-    def compute(b, c, n, lo, hi):
+    def compute(b, slot, c, n, lo, hi):
         @pl.when(odd(b))
         def _():
             def chunk(r, _):
                 for i, y in enumerate(product(both, b, c, n, r)):
                     sum1[b, c + i, r] = y.astype(jnp.bfloat16)
+                return 0
+
+            lax.fori_loop(lo, hi, chunk, 0, unroll=True)
+            for r in range(lo, hi):
+                for i in range(n):
                     first_copy(b, c + i, r).start()
-                return 0
-
-            lax.fori_loop(lo, hi, chunk, 0, unroll=True)
 
         @pl.when(jnp.logical_not(odd(b)))
         def _():
             def chunk(r, _):
                 for i, y in enumerate(product(both, b, c, n, r)):
-                    tmp[c + i, r] = y
+                    tmp[slot, c + i, r] = y
                 return 0
 
             lax.fori_loop(lo, hi, chunk, 0, unroll=True)
 
-    def settle(b, c, lo, hi):
+    def settle(b, slot, c, lo, hi):
         @pl.when(jnp.logical_not(odd(b)))
         def _():
             home = b // groups == h
@@ -284,7 +291,7 @@
 
             def one(r, _):
                 first_copy(b, c, r).wait_recv()
-                y = tmp[c, r] + sum1[b, c, r].astype(jnp.float32)
+                y = tmp[slot, c, r] + sum1[b, c, r].astype(jnp.float32)
 
                 @pl.when(home)
                 def _():
@@ -299,28 +306,36 @@
 
             lax.fori_loop(lo, hi, one, 0)
 
-    def block_side(b, side):
-        lo, hi = side * per_side, (side + 1) * per_side
-
-        def first(k, _):
-            compute(b, k * wide, wide, lo, hi)
-            return 0
-
-        def second(c, _):
-            settle(b, c, lo, hi)
-            return 0
-
-        lax.fori_loop(0, pieces // wide, first, 0)
-        lax.fori_loop(0, pieces, second, 0)
+    def early_compute(e, side):
+        b, exists, _, _ = block_at(e)
+
+        @pl.when(exists)
+        def _():
+            def one(k, _):
+                compute(b, e, k * wide, wide, side * per_side, (side + 1) * per_side)
+                return 0
+
+            lax.fori_loop(0, pieces // wide, one, 0)
+
+    def early_settle(e, side):
+        b, exists, _, _ = block_at(e)
+
+        @pl.when(exists)
+        def _():
+            def one(c, _):
+                settle(b, e, c, side * per_side, (side + 1) * per_side)
+                return 0
+
+            lax.fori_loop(0, pieces, one, 0)
 
     def lent_first(c, r):
-        return copy(lsum1.at[c, r], lsum1.at[c, r], l1_send.at[c, r], l1_recv.at[c, r], s, near)
+        return copy(lsum1.at[c, r], lsum1.at[c, r], l1_send.at[0], l1_recv.at[c, r], s, near)
 
     def lent_result(c, r):
-        return copy(lsum2.at[c, r], lgot.at[c, r], l2_send.at[c, r], l2_recv.at[c, r], right, h)
+        return copy(lsum2.at[c, r], lgot.at[c, r], l2_send.at[0], l2_recv.at[c, r], right, h)
 
     def lent_second(c, r):
-        return copy(lgot.at[c, r], sum2.at[0, c, r], s2_send.at[0, c, r], s2_recv.at[0, c, r], s, far)
+        return copy(lgot.at[c, r], sum2.at[0, c, r], s2_send.at[0], s2_recv.at[0, c, r], s, far)
 
     def help_step(c, side):
         at = side * per_side
@@ -329,26 +344,27 @@
         def _():
             def chunk(r, _):
                 lsum1[c, r] = product(lent, 0, c, 1, r)[0].astype(jnp.bfloat16)
+                return 0
+
+            lax.fori_loop(at, at + per_side, chunk, 0, unroll=True)
+            for r in range(at, at + per_side):
                 lent_first(c, r).start()
+
+        @pl.when(jnp.logical_not(odd(0)))
+        def _():
+            def chunk(r, _):
+                tmp[4, c, r] = product(lent, 0, c, 1, r)[0]
                 return 0
 
             lax.fori_loop(at, at + per_side, chunk, 0, unroll=True)
 
-        @pl.when(jnp.logical_not(odd(0)))
-        def _():
-            def chunk(r, _):
-                tmp[c, r] = product(lent, 0, c, 1, r)[0]
-                return 0
-
-            lax.fori_loop(at, at + per_side, chunk, 0, unroll=True)
-
-            def settle(r, _):
+            def add(r, _):
                 lent_first(c, r).wait_recv()
-                lsum2[c, r] = (tmp[c, r] + lsum1[c, r].astype(jnp.float32)).astype(jnp.bfloat16)
+                lsum2[c, r] = (tmp[4, c, r] + lsum1[c, r].astype(jnp.float32)).astype(jnp.bfloat16)
                 lent_result(c, r).start()
                 return 0
 
-            lax.fori_loop(at, at + per_side, settle, 0)
+            lax.fori_loop(at, at + per_side, add, 0)
 
     def in_order(one):
         def early(side):
@@ -364,19 +380,11 @@
             one(pieces - 1, side)
 
     def take_lent(c, side):
-        @pl.when(jnp.logical_not(odd(0)))
+        @pl.when(jnp.logical_not(odd(0)) & (h != 0))
         def _():
             def each(r, _):
                 lent_result(c, r).wait_recv()
-
-                @pl.when(h == 0)
-                def _():
-                    keep[0, c, r] = lgot[c, r].astype(jnp.float32)
-
-                @pl.when(h != 0)
-                def _():
-                    lent_second(c, r).start()
-
+                lent_second(c, r).start()
                 return 0
 
             lax.fori_loop(side * per_side, (side + 1) * per_side, each, 0)
@@ -402,15 +410,16 @@
             def _():
                 take_early(c)
 
-        b, exists, _, _ = block_at(e)
-
-        @pl.when(exists)
-        def _():
-            block_side(b, 1)
+        early_compute(e, 1)
+
+        @pl.when(e > 0)
+        def _():
+            early_settle(e - 1, 1)
 
         return 0
 
     lax.fori_loop(0, 4, own_side, 0)
+    early_settle(3, 1)
 
     for j in range(2):
         attn_copy(j).wait_recv()
@@ -420,11 +429,7 @@
                 lend_other(0, both.at[0, 0], left).start()
 
     def other_side(e, _):
-        b, exists, _, _ = block_at(e)
-
-        @pl.when(exists)
-        def _():
-            block_side(b, 0)
+        early_compute(e, 0)
 
         @pl.when(is_helper & (e == 0))
         def _():
@@ -432,9 +437,14 @@
                 lend_own(j).wait_recv()
             lend_other(1, lent.at[1, 1], mate).start()
 
+        @pl.when(e > 0)
+        def _():
+            early_settle(e - 1, 0)
+
         return 0
 
     lax.fori_loop(0, 4, other_side, 0)
+    early_settle(3, 0)
 
     def block_step(e, _):
         b, exists, from_up, d = block_at(e)
@@ -452,6 +462,10 @@
                 def _():
                     take_right(d - 1, c)
 
+                @pl.when(helping & (c < pieces - 1))
+                def _():
+                    help_step(c, 1)
+
                 @pl.when(helping & (c == pieces - 1))
                 def _():
                     for j in range(2):
@@ -464,13 +478,8 @@
                     lax.fori_loop(0, pieces, other, 0)
                     help_step(c, 1)
 
-                compute(b, c, 1, 0, CHUNKS)
-                settle(b, c, 0, CHUNKS)
-
-                @pl.when(helping & (c < pieces - 1))
-                def _():
-                    help_step(c, 1)
-
+                compute(b, 4, c, 1, 0, CHUNKS)
+                settle(b, 4, c, 0, CHUNKS)
                 return 0
 
             lax.fori_loop(0, pieces, one, 0)
@@ -483,25 +492,47 @@
 
     lax.fori_loop(4, 2 * pairs - 1, block_step, 0)
 
-    def result(g, c, r):
-        b = h * groups + g
-        second_copy(b, c, r).wait_recv()
-        return (keep[g, c, r] + sum2[b, c, r].astype(jnp.float32)).astype(jnp.bfloat16)
+    def result(g, c, r, store):
+        def usual():
+            second_copy(h * groups + g, c, r).wait_recv()
+            store((keep[g, c, r] + sum2[h * groups + g, c, r].astype(jnp.float32)).astype(jnp.bfloat16))
+
+        if g > 0:
+            usual()
+            return
+        helped = is_last & (h == 0)
+        pl.when(jnp.logical_not(helped))(usual)
+
+        @pl.when(helped)
+        def _():
+            lent_result(c, r).wait_recv()
+            second_copy(0, c, r).wait_recv()
+            store((lgot[c, r].astype(jnp.float32) + sum2[0, c, r].astype(jnp.float32)).astype(jnp.bfloat16))
+
+    def columns(g, c, member):
+        return pl.ds(pl.multiple_of((2 * g + member) * wc + c * wcp, wcp), wcp)
 
     def place(g, c, r, member, value):
         at = pl.multiple_of(lax.rem(r, per_side) * part, part)
-        first_col = pl.multiple_of((2 * g + member) * wc + c * wcp, wcp)
-        out_ref[pl.ds(at, part), pl.ds(first_col, wcp)] = value
+        out_ref[pl.ds(at, part), columns(g, c, member)] = value
+
+    def out_copy(g, c, member):
+        cols = columns(g, c, member)
+        return pltpu.make_async_copy(out_ref.at[:, cols], out_hbm.at[:, cols], out_sem.at[0])
 
     for g in range(groups):
         def pass_on(c, side):
             for r in range(side * per_side, (side + 1) * per_side):
-                value = result(g, c, r)
-                if side:
-                    place(g, c, r, m, value)
-                else:
-                    give3[g, c, r] = value
-                    third_copy(g, c, r).start()
+                def store(value):
+                    if side:
+                        place(g, c, r, m, value)
+                    else:
+                        give3[g, c, r] = value
+                        third_copy(g, c, r).start()
+
+                result(g, c, r, store)
+            if side:
+                out_copy(g, c, m).start()
 
         in_order(pass_on)
 
@@ -510,6 +541,7 @@
             for r in range(per_side):
                 third_copy(g, c, r).wait_recv()
                 place(g, c, r, 1 - m, got3[g, c, r])
+            out_copy(g, c, 1 - m).start()
             return 0
 
         lax.fori_loop(0, pieces, take_in, 0)
@@ -542,30 +574,35 @@
 
         attn_copy(j).wait_send()
 
+    def sent(ref, sem):
+        copy(ref, ref, sem, s1_recv.at[0, 0, 0], s, near).wait_send()
+
     def drain(b, _):
-        def one(c, _):
-            @pl.when(has_down & (p + b < pairs))
-            def _():
-                left_copy(b, c).wait_send()
-
-            @pl.when(has_up & (p - b >= 0) & jnp.logical_not(is_helper & (p == b)))
-            def _():
-                right_copy(b, c).wait_send()
-
-            for r in range(CHUNKS):
-                @pl.when(odd(b) & jnp.logical_not(is_last & (b == 0)))
-                def _():
-                    first_copy(b, c, r).wait_send()
-
-                @pl.when(jnp.logical_not(odd(b)) & (b // groups != h))
-                def _():
-                    second_copy(b, c, r).wait_send()
-
-            return 0
-
-        return lax.fori_loop(0, pieces, one, 0)
+        @pl.when(has_down & (p + b < pairs))
+        def _():
+            sent(wbuf.at[b], wl_send.at[b])
+
+        @pl.when(has_up & (p - b >= 0) & jnp.logical_not(is_helper & (p == b)))
+        def _():
+            sent(wbuf.at[b], wr_send.at[b])
+
+        lent_block = is_last & (b == 0)
+
+        @pl.when(odd(b) & jnp.logical_not(lent_block))
+        def _():
+            sent(sum1.at[b], s1_send.at[b])
+
+        @pl.when(jnp.logical_not(odd(b)) & (b // groups != h) & jnp.logical_not(lent_block))
+        def _():
+            sent(sum2.at[b], s2_send.at[b])
+
+        return 0
 
     lax.fori_loop(0, pairs, drain, 0)
+    for g in range(groups):
+        sent(give3.at[g], s3_send.at[g])
+
+    pltpu.make_async_copy(out_ref, out_hbm, out_sem.at[0]).wait()
 
     @pl.when(is_last)
     def _():
@@ -573,31 +610,21 @@
             lend_own(j).wait_send()
         lend_other(0, both.at[0, 0], left).wait_send()
 
+        @pl.when(jnp.logical_not(odd(0)) & (h != 0))
+        def _():
+            sent(lgot, s2_send.at[0])
+
     @pl.when(is_helper)
     def _():
         lend_other(1, lent.at[1, 1], mate).wait_send()
 
-        def one(c, _):
-            for r in range(CHUNKS):
-                @pl.when(odd(0))
-                def _():
-                    lent_first(c, r).wait_send()
-
-                @pl.when(jnp.logical_not(odd(0)))
-                def _():
-                    lent_result(c, r).wait_send()
-
-            return 0
-
-        lax.fori_loop(0, pieces, one, 0)
-
-    for g in range(groups):
-        def sent(c, _):
-            for r in range(per_side):
-                third_copy(g, c, r).wait_send()
-            return 0
-
-        lax.fori_loop(0, pieces, sent, 0)
+        @pl.when(odd(0))
+        def _():
+            sent(lsum1, l1_send.at[0])
+
+        @pl.when(jnp.logical_not(odd(0)))
+        def _():
+            sent(lsum2, l2_send.at[0])
 
 
 def body(n_seq, queries, keys, values, doc_lengths, out_weight):
@@ -611,15 +638,16 @@
     wcp = min(PIECE, wc)
     pieces = wc // wcp
     slots = -(-(MOST - 1) // rows) + 1
-    vmem = pl.BlockSpec(memory_space=pltpu.VMEM)
     hbm = pl.BlockSpec(memory_space=pl.ANY)
     bf, f32, dma = jnp.bfloat16, jnp.float32, pltpu.SemaphoreType.DMA
     return pl.pallas_call(
         functools.partial(kernel, n_seq),
         out_shape=jax.ShapeDtypeStruct((rows, wc * 2 * (pairs // 4)), bf),
-        in_specs=[pl.BlockSpec(memory_space=pltpu.SMEM), vmem, hbm, hbm, hbm],
-        out_specs=vmem,
+        in_specs=[pl.BlockSpec(memory_space=pltpu.SMEM), hbm, hbm, hbm, hbm],
+        out_specs=hbm,
         scratch_shapes=[
+            pltpu.VMEM((rows, width), bf),
+            pltpu.VMEM((rows, wc * 2 * groups), bf),
             pltpu.VMEM((slots, rows, kv_width), bf),
             pltpu.VMEM((slots, rows, kv_width), bf),
             pltpu.VMEM((pairs, pieces, depth, wcp), bf),
@@ -629,7 +657,7 @@
             pltpu.VMEM((heads, 1, rows), f32),
             pltpu.VMEM((heads, DH, rows), f32),
             pltpu.VMEM((2, 2, rows, width // 2), bf),
-            pltpu.VMEM((pieces, CHUNKS, part, wcp), f32),
+            pltpu.VMEM((5, pieces, CHUNKS, part, wcp), f32),
             pltpu.VMEM((groups, pieces, CHUNKS, part, wcp), f32),
             pltpu.VMEM((pairs, pieces, CHUNKS, part, wcp), bf),
             pltpu.VMEM((pairs, pieces, CHUNKS, part, wcp), bf),
@@ -639,14 +667,13 @@
             pltpu.VMEM((pieces, CHUNKS, part, wcp), bf),
             pltpu.VMEM((pieces, CHUNKS, part, wcp), bf),
             pltpu.VMEM((pieces, CHUNKS, part, wcp), bf),
-            dma((2 + pieces,)), dma((2, 2, 2)), dma((3, 2, 2)), dma((slots, 2, 2)),
-            dma((pairs, pieces)), dma((pairs, pieces)), dma((pairs, pieces)), dma((pairs, pieces)),
-            dma((2,)), dma((2,)),
-            dma((pairs, pieces, CHUNKS)), dma((pairs, pieces, CHUNKS)),
-            dma((pairs, pieces, CHUNKS)), dma((pairs, pieces, CHUNKS)),
-            dma((groups, pieces, CHUNKS // 2)), dma((groups, pieces, CHUNKS // 2)),
-            dma((2, 2)), dma((2, 2)), dma((pieces, CHUNKS)), dma((pieces, CHUNKS)),
-            dma((pieces, CHUNKS)), dma((pieces, CHUNKS)),
+            dma((3 + pieces,)), dma((1,)), dma((2, 2, 2)), dma((3, 2, 2)), dma((slots, 2, 2)),
+            dma((pairs,)), dma((pairs, pieces)), dma((pairs,)), dma((pairs, pieces)),
+            dma((2,)), dma((2,)), dma((pairs,)), dma((pairs, pieces, CHUNKS)),
+            dma((pairs,)), dma((pairs, pieces, CHUNKS)),
+            dma((groups,)), dma((groups, pieces, CHUNKS // 2)),
+            dma((2, 2)), dma((2, 2)), dma((1,)), dma((pieces, CHUNKS)),
+            dma((1,)), dma((pieces, CHUNKS)),
         ],
         compiler_params=pltpu.CompilerParams(
             collective_id=0, has_side_effects=True, vmem_limit_bytes=56 * 1024 * 1024

time: 99.5 us -> 96.4 us (0.969)
  Pallas kernels: 97.1 us -> 93.9 us
    pallas_call x1, Pallas kernels: 97.1 us -> 93.9 us  [body(): pl.pallas_call(functools.partial(kernel, n_seq), out_shape=jax.ShapeDtype...]
where the time goes in v3:
time: 96.4 us; the launch traced here: 96.2 us
  Pallas kernels  93.9 us (97%)
  local copies, waits for them, and re-layouts  2.26 us (2%)
    pallas_call x1, Pallas kernels, body(): pl.pallas_call(functools.partial(kernel, n_seq), out_shape=jax.ShapeDtype...  93.9 us
    unnamed x1, local copies, waits for them, and re-layouts  2.26 us

profile of v3, /device:TPU:24, one launch (start us, length us, event | category | flops | bytes accessed | tf_op | source)
XLA Modules:
  0.0 96.2 jit_solution(13725931600128096231)
XLA Ops:
  0.0 93.9 %shard_map.55 = bf16[512,1024]{1,0:T(8,128)(2,1)} custom-call(s32[16]{0:T(128)} %lens_ref.1, bf16[512,1024]{1,0:T(8,128)(2,1)} %q_hbm.1, bf16[512,256]{1,0:T(8,128)(2,1)} %k_hbm.1, bf16[512,256]{1,0:T(8,128)(2,1)} %v_hbm.1, bf16[1024,512]{1,0:T(8,128)(2,1)} %w_hbm.1), custom_call_target="tpu_custom_call" | custom-call | tf_op jit(solution)/shard_map/pallas_call | solution.py:643
  93.9 2.3 %copy.7 = bf16[512,1024]{1,0:T(8,128)(2,1)} copy(bf16[512,1024]{1,0:T(8,128)(2,1)} %shard_map.55) | data formatting | bytes 2097152

commit v4 on v3

--- a/solution.py
+++ b/solution.py
@@ -19,7 +19,7 @@
 
 def kernel(
     n_seq, lens_ref, q_hbm, k_hbm, v_hbm, w_hbm, out_hbm,
-    q_ref, out_ref, kbuf, vbuf, wbuf, bias, vt, mx, sm, acc, both,
+    q_ref, out_ref, kvbuf, wbuf, bias, vt, mx, sm, acc, both,
     tmp, keep, sum1, sum2, give3, got3, lent, lsum1, lsum2, lgot,
     load_sem, out_sem, kvz_send, kvy_send, kv_recv, wl_send, wl_recv, wr_send, wr_recv,
     at_send, at_recv, s1_send, s1_recv, s2_send, s2_recv, s3_send, s3_recv,
@@ -41,6 +41,7 @@
     group_size = HQ // KV
     part = rows * 2 // CHUNKS
     wide = 2 if pieces % 2 == 0 else 1
+    split = pieces // 2 if pieces % (2 * wide) == 0 else pieces
     has_up, has_down = p + 1 < pairs, p >= 1
     is_last, is_helper = p == pairs - 1, p == pairs - 2
     scale = DH ** (-0.5) * math.log2(math.e)
@@ -51,13 +52,10 @@
             device_id={"seq": seq, "head": head}, device_id_type=MESH,
         )
 
-    def kv_copies(src_slot, dst_slot, j, send, target):
+    def kv_copy(src_slot, dst_slot, j, send, target):
         cols = pl.ds(pl.multiple_of(j * DH, DH), DH)
-        return [
-            copy(buf.at[src_slot, :, cols], buf.at[dst_slot, :, cols],
-                 send.at[j, c], kv_recv.at[dst_slot, j, c], target, h)
-            for c, buf in enumerate((kbuf, vbuf))
-        ]
+        return copy(kvbuf.at[src_slot, :, :, cols], kvbuf.at[dst_slot, :, :, cols],
+                    send.at[j], kv_recv.at[dst_slot, j], target, h)
 
     def w_copy(block, c, step, send, recv, target):
         piece = wbuf.at[block, c]
@@ -70,10 +68,10 @@
         return w_copy(jnp.maximum(p - step, 0), c, step, wr_send, wr_recv, right)
 
     loads = [
-        pltpu.make_async_copy(k_hbm, kbuf.at[0], load_sem.at[0]),
-        pltpu.make_async_copy(v_hbm, vbuf.at[0], load_sem.at[1]),
+        pltpu.make_async_copy(k_hbm, kvbuf.at[0, 0], load_sem.at[0]),
+        pltpu.make_async_copy(v_hbm, kvbuf.at[0, 1], load_sem.at[1]),
     ] + [
-        pltpu.make_async_copy(w_hbm.at[:, c * wcp:(c + 1) * wcp], wbuf.at[p, c], load_sem.at[3 + c])
+        pltpu.make_async_copy(w_hbm.at[:, c * wcp:(c + 1) * wcp], wbuf.at[p, c], load_sem.at[3])
         for c in range(pieces)
     ] + [pltpu.make_async_copy(q_hbm, q_ref, load_sem.at[2])]
     for load in loads:
@@ -90,16 +88,13 @@
     for j in range(2):
         @pl.when(has_next)
         def _():
-            for c in kv_copies(0, 2, j, kvz_send.at[0], right):
-                c.start()
+            kv_copy(0, 2, j, kvz_send.at[0], right).start()
 
         @pl.when(m == 0)
         def _():
-            for c in kv_copies(0, 1, j, kvy_send.at[0], mate):
-                c.start()
-
-    for load in loads[2:-1]:
-        load.wait()
+            kv_copy(0, 1, j, kvy_send.at[0], mate).start()
+
+    pltpu.make_async_copy(wbuf.at[p], wbuf.at[p], load_sem.at[3]).wait()
 
     @pl.when(has_down)
     def _():
@@ -158,23 +153,19 @@
 
         @pl.when((i >= 2) & (s >= slot))
         def _():
-            for c in kv_copies(slot, slot, j, kvz_send.at[0], right):
-                c.wait_recv()
+            kv_copy(slot, slot, j, kvz_send.at[0], right).wait_recv()
 
             @pl.when((slot == 2) & has_next)
             def _():
-                for c in kv_copies(2, 4, j, kvz_send.at[1], right):
-                    c.start()
+                kv_copy(2, 4, j, kvz_send.at[1], right).start()
 
             @pl.when(slot == 2)
             def _():
-                for c in kv_copies(2, 3 - 2 * m, j, kvy_send.at[1], mate):
-                    c.start()
+                kv_copy(2, 3 - 2 * m, j, kvy_send.at[1], mate).start()
 
             @pl.when((slot == 4) & (m == 1))
             def _():
-                for c in kv_copies(4, 3, j, kvy_send.at[2], mate):
-                    c.start()
+                kv_copy(4, 3, j, kvy_send.at[2], mate).start()
 
         @pl.when(i == 8)
         def _():
@@ -182,8 +173,13 @@
 
         @pl.when((i == 4) & has_up)
         def _():
-            for c in range(pieces):
+            for c in range(split):
                 right_copy(0, c).start()
+
+            @pl.when(jnp.logical_not(is_helper))
+            def _():
+                for c in range(split, pieces):
+                    right_copy(0, c).start()
 
         for c in range(pieces):
             @pl.when((i == 11 - 2 * (pieces - c)) & has_up)
@@ -195,13 +191,13 @@
             cols = pl.ds(pl.multiple_of(j * DH, DH), DH)
             k_pos = (s - slot) * rows + lax.broadcasted_iota(jnp.int32, (rows, rows), 0)
             bias[...] = jnp.where((k_pos >= first) & (k_pos <= q_pos), 0.0, -1e30)
-            vt[...] = jnp.transpose(vbuf[slot, :, cols])
+            vt[...] = jnp.transpose(kvbuf[slot, 1, :, cols])
 
             def one(g, _):
                 at = j * group_size + g
                 q = q_ref[:, pl.ds(pl.multiple_of(at * DH, DH), DH)]
                 scores = lax.dot_general(
-                    kbuf[slot, :, cols], q, (((1,), (1,)), ((), ())),
+                    kvbuf[slot, 0, :, cols], q, (((1,), (1,)), ((), ())),
                     preferred_element_type=jnp.float32,
                 ) * scale + bias[...]
                 top = jnp.max(scores, axis=0, keepdims=True)
@@ -238,14 +234,19 @@
 
     per_side = CHUNKS // 2
 
-    def first_copy(b, c, r):
-        return copy(sum1.at[b, c, r], sum1.at[b, c, r], s1_send.at[b], s1_recv.at[b, c, r], s, near)
-
-    def second_copy(b, c, r):
-        return copy(sum2.at[b, c, r], sum2.at[b, c, r], s2_send.at[b], s2_recv.at[b, c, r], s, far)
-
-    def third_copy(g, c, r):
-        return copy(give3.at[g, c, r], got3.at[g, c, r], s3_send.at[g], s3_recv.at[g, c, r], mate, h)
+    def rows_of(side):
+        return pl.ds(side * per_side, per_side)
+
+    def first_copy(b, c, side):
+        piece = sum1.at[b, c, rows_of(side)]
+        return copy(piece, piece, s1_send.at[b], s1_recv.at[b, c, side], s, near)
+
+    def second_copy(b, c, side):
+        piece = sum2.at[b, c, rows_of(side)]
+        return copy(piece, piece, s2_send.at[b], s2_recv.at[b, c, side], s, far)
+
+    def third_copy(g, c):
+        return copy(give3.at[g, c], got3.at[g, c], s3_send.at[g], s3_recv.at[g, c], mate, h)
 
     def odd(b):
         return lax.rem(b // groups + h, 2) == 1
@@ -261,7 +262,9 @@
              + jnp.dot(source[side, 1, pl.ds(at, part), :], weights(half), preferred_element_type=jnp.float32))
         return [y[:, i * wcp:(i + 1) * wcp] for i in range(n)]
 
-    def compute(b, slot, c, n, lo, hi):
+    def compute(b, slot, c, n, sides):
+        lo, hi = sides[0] * per_side, (sides[-1] + 1) * per_side
+
         @pl.when(odd(b))
         def _():
             def chunk(r, _):
@@ -270,9 +273,9 @@
                 return 0
 
             lax.fori_loop(lo, hi, chunk, 0, unroll=True)
-            for r in range(lo, hi):
+            for side in sides:
                 for i in range(n):
-                    first_copy(b, c + i, r).start()
+                    first_copy(b, c + i, side).start()
 
         @pl.when(jnp.logical_not(odd(b)))
         def _():
@@ -283,28 +286,34 @@
 
             lax.fori_loop(lo, hi, chunk, 0, unroll=True)
 
-    def settle(b, slot, c, lo, hi):
+    def settle(b, slot, c, sides):
         @pl.when(jnp.logical_not(odd(b)))
         def _():
             home = b // groups == h
             g = lax.rem(b, groups)
 
-            def one(r, _):
-                first_copy(b, c, r).wait_recv()
-                y = tmp[slot, c, r] + sum1[b, c, r].astype(jnp.float32)
+            def one(side, _):
+                first_copy(b, c, side).wait_recv()
 
                 @pl.when(home)
                 def _():
-                    keep[g, c, r] = y
+                    for k in range(per_side):
+                        r = side * per_side + k
+                        keep[g, c, r] = tmp[slot, c, r] + sum1[b, c, r].astype(jnp.float32)
 
                 @pl.when(jnp.logical_not(home))
                 def _():
-                    sum2[b, c, r] = y.astype(jnp.bfloat16)
-                    second_copy(b, c, r).start()
-
-                return 0
-
-            lax.fori_loop(lo, hi, one, 0)
+                    for k in range(per_side):
+                        r = side * per_side + k
+                        sum2[b, c, r] = (tmp[slot, c, r] + sum1[b, c, r].astype(jnp.float32)).astype(jnp.bfloat16)
+                    second_copy(b, c, side).start()
+
+                return 0
+
+            lax.fori_loop(sides[0], sides[-1] + 1, one, 0)
+
+    def early_pieces(e):
+        return jnp.where(is_last & (e == 2), split, pieces)
 
     def early_compute(e, side):
         b, exists, _, _ = block_at(e)
@@ -312,10 +321,10 @@
         @pl.when(exists)
         def _():
             def one(k, _):
-                compute(b, e, k * wide, wide, side * per_side, (side + 1) * per_side)
-                return 0
-
-            lax.fori_loop(0, pieces // wide, one, 0)
+                compute(b, e, k * wide, wide, (side,))
+                return 0
+
+            lax.fori_loop(0, early_pieces(e) // wide, one, 0)
 
     def early_settle(e, side):
         b, exists, _, _ = block_at(e)
@@ -323,19 +332,20 @@
         @pl.when(exists)
         def _():
             def one(c, _):
-                settle(b, e, c, side * per_side, (side + 1) * per_side)
-                return 0
-
-            lax.fori_loop(0, pieces, one, 0)
-
-    def lent_first(c, r):
-        return copy(lsum1.at[c, r], lsum1.at[c, r], l1_send.at[0], l1_recv.at[c, r], s, near)
+                settle(b, e, c, (side,))
+                return 0
+
+            lax.fori_loop(0, early_pieces(e), one, 0)
+
+    def lent_first(c, side):
+        piece = lsum1.at[c, rows_of(side)]
+        return copy(piece, piece, l1_send.at[0], l1_recv.at[c, side], s, near)
 
     def lent_result(c, r):
         return copy(lsum2.at[c, r], lgot.at[c, r], l2_send.at[0], l2_recv.at[c, r], right, h)
 
     def lent_second(c, r):
-        return copy(lgot.at[c, r], sum2.at[0, c, r], s2_send.at[0], s2_recv.at[0, c, r], s, far)
+        return copy(lgot.at[c, r], sum2.at[0, c, r], s2_send.at[0], s2_recv.at[0, c, r // per_side], s, far)
 
     def help_step(c, side):
         at = side * per_side
@@ -347,8 +357,7 @@
                 return 0
 
             lax.fori_loop(at, at + per_side, chunk, 0, unroll=True)
-            for r in range(at, at + per_side):
-                lent_first(c, r).start()
+            lent_first(c, side).start()
 
         @pl.when(jnp.logical_not(odd(0)))
         def _():
@@ -358,8 +367,9 @@
 
             lax.fori_loop(at, at + per_side, chunk, 0, unroll=True)
 
+            lent_first(c, side).wait_recv()
+
             def add(r, _):
-                lent_first(c, r).wait_recv()
                 lsum2[c, r] = (tmp[4, c, r] + lsum1[c, r].astype(jnp.float32)).astype(jnp.bfloat16)
                 lent_result(c, r).start()
                 return 0
@@ -380,14 +390,12 @@
             one(pieces - 1, side)
 
     def take_lent(c, side):
-        @pl.when(jnp.logical_not(odd(0)) & (h != 0))
-        def _():
-            def each(r, _):
-                lent_result(c, r).wait_recv()
-                lent_second(c, r).start()
-                return 0
-
-            lax.fori_loop(side * per_side, (side + 1) * per_side, each, 0)
+        def each(r, _):
+            lent_result(c, r).wait_recv()
+            lent_second(c, r).start()
+            return 0
+
+        lax.fori_loop(side * per_side, (side + 1) * per_side, each, 0)
 
     def block_at(e):
         d = (e + 1) // 2
@@ -396,9 +404,15 @@
         return jnp.clip(b, 0, pairs - 1), (b >= 0) & (b < pairs), from_up, d
 
     def take_early(c):
-        @pl.when(has_down)
+        @pl.when(has_down & (jnp.logical_not(is_last) | (c < split)))
         def _():
             take_right(0, c)
+
+        if c == pieces - 1:
+            @pl.when(is_helper)
+            def _():
+                for k in range(split, pieces):
+                    right_copy(0, k).start()
 
         @pl.when(p + 2 < pairs)
         def _():
@@ -428,28 +442,41 @@
             def _():
                 lend_other(0, both.at[0, 0], left).start()
 
-    def other_side(e, _):
-        early_compute(e, 0)
-
-        @pl.when(is_helper & (e == 0))
+    late = is_last | is_helper
+
+    def other_side(k, _):
+        order = (2, 1, 0, 3)
+
+        def at(k):
+            return sum(jnp.where(k == i, e, 0) for i, e in enumerate(order))
+
+        @pl.when(jnp.logical_not(late) | (is_helper & (k == 0)))
+        def _():
+            early_compute(at(k), 0)
+
+        @pl.when(is_helper & (k == 0))
         def _():
             for j in range(2):
                 lend_own(j).wait_recv()
             lend_other(1, lent.at[1, 1], mate).start()
 
-        @pl.when(e > 0)
-        def _():
-            early_settle(e - 1, 0)
+        @pl.when((jnp.logical_not(late) & (k > 0)) | (is_helper & (k == 1)))
+        def _():
+            early_settle(at(k - 1), 0)
 
         return 0
 
     lax.fori_loop(0, 4, other_side, 0)
-    early_settle(3, 0)
+
+    @pl.when(jnp.logical_not(late))
+    def _():
+        early_settle(3, 0)
 
     def block_step(e, _):
         b, exists, from_up, d = block_at(e)
         helped = is_last & (b == 0)
         helping = is_helper & (b == 0)
+        last_block = 2 * (pairs - 2)
 
         @pl.when(exists & jnp.logical_not(helped))
         def _():
@@ -478,24 +505,57 @@
                     lax.fori_loop(0, pieces, other, 0)
                     help_step(c, 1)
 
-                compute(b, 4, c, 1, 0, CHUNKS)
-                settle(b, 4, c, 0, CHUNKS)
+                compute(b, 4, c, 1, (0, 1))
+                settle(b, 4, c, (0, 1))
+
+                @pl.when(late & (e == last_block) & (c == min(1, pieces - 1)))
+                def _():
+                    early_compute(0, 0)
+
+                    @pl.when(is_helper)
+                    def _():
+                        early_compute(1, 0)
+
+                    @pl.when(is_last)
+                    def _():
+                        early_compute(2, 0)
+
+                    early_settle(0, 0)
+
+                    @pl.when(is_helper)
+                    def _():
+                        early_settle(1, 0)
+
+                    @pl.when(is_last)
+                    def _():
+                        early_settle(2, 0)
+
                 return 0
 
             lax.fori_loop(0, pieces, one, 0)
 
-        @pl.when(helped)
-        def _():
-            in_order(take_lent)
+        @pl.when(is_last & (e == 4))
+        def _():
+            def rest(c, _):
+                take_right(0, c)
+                compute(p - 1, 4, c, 1, (0, 1))
+                settle(p - 1, 4, c, (0, 1))
+                return 0
+
+            lax.fori_loop(split, pieces, rest, 0)
 
         return 0
 
     lax.fori_loop(4, 2 * pairs - 1, block_step, 0)
 
-    def result(g, c, r, store):
+    def result(g, c, side, store):
+        b = h * groups + g
+        at = [side * per_side + k for k in range(per_side)]
+
         def usual():
-            second_copy(h * groups + g, c, r).wait_recv()
-            store((keep[g, c, r] + sum2[h * groups + g, c, r].astype(jnp.float32)).astype(jnp.bfloat16))
+            second_copy(b, c, side).wait_recv()
+            for r in at:
+                store(r, (keep[g, c, r] + sum2[b, c, r].astype(jnp.float32)).astype(jnp.bfloat16))
 
         if g > 0:
             usual()
@@ -505,9 +565,11 @@
 
         @pl.when(helped)
         def _():
-            lent_result(c, r).wait_recv()
-            second_copy(0, c, r).wait_recv()
-            store((lgot[c, r].astype(jnp.float32) + sum2[0, c, r].astype(jnp.float32)).astype(jnp.bfloat16))
+            for r in at:
+                lent_result(c, r).wait_recv()
+            second_copy(0, c, side).wait_recv()
+            for r in at:
+                store(r, (lgot[c, r].astype(jnp.float32) + sum2[0, c, r].astype(jnp.float32)).astype(jnp.bfloat16))
 
     def columns(g, c, member):
         return pl.ds(pl.multiple_of((2 * g + member) * wc + c * wcp, wcp), wcp)
@@ -520,26 +582,47 @@
         cols = columns(g, c, member)
         return pltpu.make_async_copy(out_ref.at[:, cols], out_hbm.at[:, cols], out_sem.at[0])
 
-    for g in range(groups):
-        def pass_on(c, side):
-            for r in range(side * per_side, (side + 1) * per_side):
-                def store(value):
-                    if side:
-                        place(g, c, r, m, value)
-                    else:
-                        give3[g, c, r] = value
-                        third_copy(g, c, r).start()
-
-                result(g, c, r, store)
+    def pass_on(c, side):
+        for g in range(groups):
+            def store(r, value):
+                if side:
+                    place(g, c, r, m, value)
+                else:
+                    give3[g, c, r] = value
+
+            result(g, c, side, store)
             if side:
                 out_copy(g, c, m).start()
-
+            else:
+                third_copy(g, c).start()
+
+    lender = is_last & jnp.logical_not(odd(0)) & (h != 0)
+
+    @pl.when(lender)
+    def _():
+        def each(one, sides):
+            def body(c, _):
+                for side in sides:
+                    one(c, side)
+                return 0
+
+            lax.fori_loop(0, pieces - 1, body, 0)
+
+        each(take_lent, (1,))
+        each(pass_on, (0, 1))
+        each(take_lent, (0,))
+        for one in (pass_on, take_lent):
+            for side in range(2):
+                one(pieces - 1, side)
+
+    @pl.when(jnp.logical_not(lender))
+    def _():
         in_order(pass_on)
 
     for g in range(groups):
         def take_in(c, _):
+            third_copy(g, c).wait_recv()
             for r in range(per_side):
-                third_copy(g, c, r).wait_recv()
                 place(g, c, r, 1 - m, got3[g, c, r])
             out_copy(g, c, 1 - m).start()
             return 0
@@ -549,28 +632,23 @@
     for j in range(2):
         @pl.when(has_next)
         def _():
-            for c in kv_copies(0, 2, j, kvz_send.at[0], right):
-                c.wait_send()
+            kv_copy(0, 2, j, kvz_send.at[0], right).wait_send()
 
         @pl.when((s >= 2) & has_next)
         def _():
-            for c in kv_copies(2, 4, j, kvz_send.at[1], right):
-                c.wait_send()
+            kv_copy(2, 4, j, kvz_send.at[1], right).wait_send()
 
         @pl.when(m == 0)
         def _():
-            for c in kv_copies(0, 1, j, kvy_send.at[0], mate):
-                c.wait_send()
+            kv_copy(0, 1, j, kvy_send.at[0], mate).wait_send()
 
         @pl.when(s >= 2)
         def _():
-            for c in kv_copies(2, 3 - 2 * m, j, kvy_send.at[1], mate):
-                c.wait_send()
+            kv_copy(2, 3 - 2 * m, j, kvy_send.at[1], mate).wait_send()
 
         @pl.when((s >= 4) & (m == 1))
         def _():
-            for c in kv_copies(4, 3, j, kvy_send.at[2], mate):
-                c.wait_send()
+            kv_copy(4, 3, j, kvy_send.at[2], mate).wait_send()
 
         attn_copy(j).wait_send()
 
@@ -648,8 +726,7 @@
         scratch_shapes=[
             pltpu.VMEM((rows, width), bf),
             pltpu.VMEM((rows, wc * 2 * groups), bf),
-            pltpu.VMEM((slots, rows, kv_width), bf),
-            pltpu.VMEM((slots, rows, kv_width), bf),
+            pltpu.VMEM((slots, 2, rows, kv_width), bf),
             pltpu.VMEM((pairs, pieces, depth, wcp), bf),
             pltpu.VMEM((rows, rows), f32),
             pltpu.VMEM((DH, rows), bf),
@@ -667,13 +744,11 @@
             pltpu.VMEM((pieces, CHUNKS, part, wcp), bf),
             pltpu.VMEM((pieces, CHUNKS, part, wcp), bf),
             pltpu.VMEM((pieces, CHUNKS, part, wcp), bf),
-            dma((3 + pieces,)), dma((1,)), dma((2, 2, 2)), dma((3, 2, 2)), dma((slots, 2, 2)),
-            dma((pairs,)), dma((pairs, pieces)), dma((pairs,)), dma((pairs, pieces)),
-            dma((2,)), dma((2,)), dma((pairs,)), dma((pairs, pieces, CHUNKS)),
-            dma((pairs,)), dma((pairs, pieces, CHUNKS)),
-            dma((groups,)), dma((groups, pieces, CHUNKS // 2)),
-            dma((2, 2)), dma((2, 2)), dma((1,)), dma((pieces, CHUNKS)),
-            dma((1,)), dma((pieces, CHUNKS)),
+            dma((4,)), dma((1,)), dma((2, 2)), dma((3, 2)), dma((slots, 2)),
+            dma((pairs - 1,)), dma((pairs - 1, pieces)), dma((pairs - 1,)), dma((pairs - 1, pieces)),
+            dma((2,)), dma((2,)), dma((pairs,)), dma((pairs, pieces, 2)), dma((pairs,)), dma((pairs, pieces, 2)),
+            dma((groups,)), dma((groups, pieces)),
+            dma((2, 2)), dma((2, 2)), dma((1,)), dma((pieces, 2)), dma((1,)), dma((pieces, CHUNKS)),
         ],
         compiler_params=pltpu.CompilerParams(
             collective_id=0, has_side_effects=True, vmem_limit_bytes=56 * 1024 * 1024

time: 96.4 us -> 93.5 us (0.970)
  Pallas kernels: 93.9 us -> 91 us
    pallas_call x1, Pallas kernels: 93.9 us -> 91 us  [body(): pl.pallas_call(functools.partial(kernel, n_seq), out_shape=jax.ShapeDtype...]
where the time goes in v4:
time: 93.5 us; the launch traced here: 93.3 us
  Pallas kernels  91 us (97%)
  local copies, waits for them, and re-layouts  2.26 us (2%)
    pallas_call x1, Pallas kernels, body(): pl.pallas_call(functools.partial(kernel, n_seq), out_shape=jax.ShapeDtype...  91 us
    unnamed x1, local copies, waits for them, and re-layouts  2.26 us

profile of v4, /device:TPU:24, one launch (start us, length us, event | category | flops | bytes accessed | tf_op | source)
XLA Modules:
  0.0 93.3 jit_solution(6454676805880764192)
XLA Ops:
  0.0 91.0 %shard_map.55 = bf16[512,1024]{1,0:T(8,128)(2,1)} custom-call(s32[16]{0:T(128)} %lens_ref.1, bf16[512,1024]{1,0:T(8,128)(2,1)} %q_hbm.1, bf16[512,256]{1,0:T(8,128)(2,1)} %k_hbm.1, bf16[512,256]{1,0:T(8,128)(2,1)} %v_hbm.1, bf16[1024,512]{1,0:T(8,128)(2,1)} %w_hbm.1), custom_call_target="tpu_custom_call" | custom-call | tf_op jit(solution)/shard_map/pallas_call | solution.py:721
  91.0 2.3 %copy.7 = bf16[512,1024]{1,0:T(8,128)(2,1)} copy(bf16[512,1024]{1,0:T(8,128)(2,1)} %shard_map.55) | data formatting | bytes 2097152

commit v5 on v4

--- a/solution.py
+++ b/solution.py
@@ -376,18 +376,19 @@
 
             lax.fori_loop(at, at + per_side, add, 0)
 
+    lead = 1 if pieces > 1 else 0
+
+    def over(one, side, lo, hi):
+        def body(c, _):
+            one(c, side)
+            return 0
+
+        lax.fori_loop(lo, hi, body, 0)
+
     def in_order(one):
-        def early(side):
-            def each(c, _):
-                one(c, side)
-                return 0
-
-            lax.fori_loop(0, pieces - 1, each, 0)
-
-        early(1)
-        early(0)
-        for side in range(2):
-            one(pieces - 1, side)
+        over(one, 1, 0, lead)
+        over(one, 0, 0, pieces)
+        over(one, 1, lead, pieces)
 
     def take_lent(c, side):
         def each(r, _):
@@ -489,7 +490,7 @@
                 def _():
                     take_right(d - 1, c)
 
-                @pl.when(helping & (c < pieces - 1))
+                @pl.when(helping & (c < lead))
                 def _():
                     help_step(c, 1)
 
@@ -497,16 +498,14 @@
                 def _():
                     for j in range(2):
                         lend_other(j, both.at[0, 0], left).wait_recv()
-
-                    def other(k, _):
-                        help_step(k, 0)
-                        return 0
-
-                    lax.fori_loop(0, pieces, other, 0)
-                    help_step(c, 1)
+                    over(help_step, 0, 0, pieces)
 
                 compute(b, 4, c, 1, (0, 1))
                 settle(b, 4, c, (0, 1))
+
+                @pl.when(helping & (c == pieces - 1))
+                def _():
+                    over(help_step, 1, lead, pieces)
 
                 @pl.when(late & (e == last_block) & (c == min(1, pieces - 1)))
                 def _():
@@ -600,24 +599,28 @@
 
     @pl.when(lender)
     def _():
-        def each(one, sides):
-            def body(c, _):
-                for side in sides:
-                    one(c, side)
-                return 0
-
-            lax.fori_loop(0, pieces - 1, body, 0)
-
-        each(take_lent, (1,))
-        each(pass_on, (0, 1))
-        each(take_lent, (0,))
-        for one in (pass_on, take_lent):
-            for side in range(2):
-                one(pieces - 1, side)
-
-    @pl.when(jnp.logical_not(lender))
+        over(take_lent, 1, 0, lead)
+        for side in range(2):
+            over(pass_on, side, 0, pieces - 1)
+        over(take_lent, 0, 0, pieces)
+        for side in range(2):
+            pass_on(pieces - 1, side)
+        over(take_lent, 1, lead, pieces)
+
+    lent_to = is_last & (h == 0)
+
+    @pl.when(lent_to)
     def _():
         in_order(pass_on)
+
+    @pl.when(jnp.logical_not(lender | lent_to))
+    def _():
+        def each(c, _):
+            pass_on(c, 0)
+            pass_on(c, 1)
+            return 0
+
+        lax.fori_loop(0, pieces, each, 0)
 
     for g in range(groups):
         def take_in(c, _):

time: 93.5 us -> 92.6 us (level)
  no operation moved by 1% of the time
where the time goes in v5:
time: 92.6 us; the launch traced here: 92.5 us
  Pallas kernels  90.2 us (97%)
  local copies, waits for them, and re-layouts  2.26 us (2%)
    pallas_call x1, Pallas kernels, body(): pl.pallas_call(functools.partial(kernel, n_seq), out_shape=jax.ShapeDtype...  90.2 us
    unnamed x1, local copies, waits for them, and re-layouts  2.26 us

profile of v5, /device:TPU:24, one launch (start us, length us, event | category | flops | bytes accessed | tf_op | source)
XLA Modules:
  0.0 92.5 jit_solution(17326906655583596905)
XLA Ops:
  0.0 90.2 %shard_map.55 = bf16[512,1024]{1,0:T(8,128)(2,1)} custom-call(s32[16]{0:T(128)} %lens_ref.1, bf16[512,1024]{1,0:T(8,128)(2,1)} %q_hbm.1, bf16[512,256]{1,0:T(8,128)(2,1)} %k_hbm.1, bf16[512,256]{1,0:T(8,128)(2,1)} %v_hbm.1, bf16[1024,512]{1,0:T(8,128)(2,1)} %w_hbm.1), custom_call_target="tpu_custom_call" | custom-call | tf_op jit(solution)/shard_map/pallas_call | solution.py:724
  90.2 2.3 %copy.7 = bf16[512,1024]{1,0:T(8,128)(2,1)} copy(bf16[512,1024]{1,0:T(8,128)(2,1)} %shard_map.55) | data formatting | bytes 2097152

commit v6 on v5

--- a/solution.py
+++ b/solution.py
@@ -78,9 +78,23 @@
         load.start()
 
     barrier = pltpu.get_barrier_semaphore()
-    for seq, head in ((mate, h), (left, h), (right, h), (s, near), (s, far)):
+
+    def greet(seq, head):
         pl.semaphore_signal(barrier, inc=1, device_id={"seq": seq, "head": head}, device_id_type=MESH)
-    pl.semaphore_wait(barrier, 5)
+
+    for seq, head in ((mate, h), (s, near), (s, far)):
+        greet(seq, head)
+    for there, seq in ((has_down, left), (has_up, right)):
+        @pl.when(there)
+        def _():
+            greet(seq, h)
+
+    @pl.when(is_last)
+    def _():
+        greet(left, far)
+
+    greeted = 3 + sum(jnp.where(there, 1, 0) for there in (has_up, has_down, is_helper))
+    pl.semaphore_wait(barrier, greeted)
 
     loads[0].wait()
     loads[1].wait()
@@ -344,8 +358,8 @@
     def lent_result(c, r):
         return copy(lsum2.at[c, r], lgot.at[c, r], l2_send.at[0], l2_recv.at[c, r], right, h)
 
-    def lent_second(c, r):
-        return copy(lgot.at[c, r], sum2.at[0, c, r], s2_send.at[0], s2_recv.at[0, c, r // per_side], s, far)
+    def lent_across(c, r):
+        return copy(lsum2.at[c, r], sum2.at[0, c, r], l2_send.at[0], s2_recv.at[0, c, r // per_side], right, far)
 
     def help_step(c, side):
         at = side * per_side
@@ -371,7 +385,15 @@
 
             def add(r, _):
                 lsum2[c, r] = (tmp[4, c, r] + lsum1[c, r].astype(jnp.float32)).astype(jnp.bfloat16)
-                lent_result(c, r).start()
+
+                @pl.when(h == 0)
+                def _():
+                    lent_result(c, r).start()
+
+                @pl.when(h != 0)
+                def _():
+                    lent_across(c, r).start()
+
                 return 0
 
             lax.fori_loop(at, at + per_side, add, 0)
@@ -389,14 +411,6 @@
         over(one, 1, 0, lead)
         over(one, 0, 0, pieces)
         over(one, 1, lead, pieces)
-
-    def take_lent(c, side):
-        def each(r, _):
-            lent_result(c, r).wait_recv()
-            lent_second(c, r).start()
-            return 0
-
-        lax.fori_loop(side * per_side, (side + 1) * per_side, each, 0)
 
     def block_at(e):
         d = (e + 1) // 2
@@ -443,7 +457,7 @@
             def _():
                 lend_other(0, both.at[0, 0], left).start()
 
-    late = is_last | is_helper
+    late = is_last
 
     def other_side(k, _):
         order = (2, 1, 0, 3)
@@ -451,7 +465,7 @@
         def at(k):
             return sum(jnp.where(k == i, e, 0) for i, e in enumerate(order))
 
-        @pl.when(jnp.logical_not(late) | (is_helper & (k == 0)))
+        @pl.when(jnp.logical_not(late))
         def _():
             early_compute(at(k), 0)
 
@@ -461,7 +475,7 @@
                 lend_own(j).wait_recv()
             lend_other(1, lent.at[1, 1], mate).start()
 
-        @pl.when((jnp.logical_not(late) & (k > 0)) | (is_helper & (k == 1)))
+        @pl.when(jnp.logical_not(late) & (k > 0))
         def _():
             early_settle(at(k - 1), 0)
 
@@ -472,80 +486,6 @@
     @pl.when(jnp.logical_not(late))
     def _():
         early_settle(3, 0)
-
-    def block_step(e, _):
-        b, exists, from_up, d = block_at(e)
-        helped = is_last & (b == 0)
-        helping = is_helper & (b == 0)
-        last_block = 2 * (pairs - 2)
-
-        @pl.when(exists & jnp.logical_not(helped))
-        def _():
-            def one(c, _):
-                @pl.when(from_up)
-                def _():
-                    take_left(d - 1, c)
-
-                @pl.when(jnp.logical_not(from_up))
-                def _():
-                    take_right(d - 1, c)
-
-                @pl.when(helping & (c < lead))
-                def _():
-                    help_step(c, 1)
-
-                @pl.when(helping & (c == pieces - 1))
-                def _():
-                    for j in range(2):
-                        lend_other(j, both.at[0, 0], left).wait_recv()
-                    over(help_step, 0, 0, pieces)
-
-                compute(b, 4, c, 1, (0, 1))
-                settle(b, 4, c, (0, 1))
-
-                @pl.when(helping & (c == pieces - 1))
-                def _():
-                    over(help_step, 1, lead, pieces)
-
-                @pl.when(late & (e == last_block) & (c == min(1, pieces - 1)))
-                def _():
-                    early_compute(0, 0)
-
-                    @pl.when(is_helper)
-                    def _():
-                        early_compute(1, 0)
-
-                    @pl.when(is_last)
-                    def _():
-                        early_compute(2, 0)
-
-                    early_settle(0, 0)
-
-                    @pl.when(is_helper)
-                    def _():
-                        early_settle(1, 0)
-
-                    @pl.when(is_last)
-                    def _():
-                        early_settle(2, 0)
-
-                return 0
-
-            lax.fori_loop(0, pieces, one, 0)
-
-        @pl.when(is_last & (e == 4))
-        def _():
-            def rest(c, _):
-                take_right(0, c)
-                compute(p - 1, 4, c, 1, (0, 1))
-                settle(p - 1, 4, c, (0, 1))
-                return 0
-
-            lax.fori_loop(split, pieces, rest, 0)
-
-        return 0
-
-    lax.fori_loop(4, 2 * pairs - 1, block_step, 0)
 
     def result(g, c, side, store):
         b = h * groups + g
@@ -595,17 +535,87 @@
             else:
                 third_copy(g, c).start()
 
-    lender = is_last & jnp.logical_not(odd(0)) & (h != 0)
-
-    @pl.when(lender)
+    def pass_both(c, _):
+        pass_on(c, 0)
+        pass_on(c, 1)
+        return 0
+
+    lowest, highest = h * groups, h * groups + groups - 1
+    passed = (p < pairs - 2) & (lowest >= p - 1) & (highest <= p + 2)
+    ready = is_helper & odd(0) & (lowest <= p - 1) & (highest >= p - 1) & (groups == 1)
+
+    soon = is_helper & (lowest >= p) & (groups == 1)
+    soon_pieces = max(pieces - 2, 0)
+
+    @pl.when(passed)
     def _():
-        over(take_lent, 1, 0, lead)
-        for side in range(2):
-            over(pass_on, side, 0, pieces - 1)
-        over(take_lent, 0, 0, pieces)
-        for side in range(2):
-            pass_on(pieces - 1, side)
-        over(take_lent, 1, lead, pieces)
+        lax.fori_loop(0, pieces, pass_both, 0)
+
+    def block_step(e, _):
+        b, exists, from_up, d = block_at(e)
+        helped = is_last & (b == 0)
+        helping = is_helper & (b == 0)
+
+        @pl.when(exists & jnp.logical_not(helped))
+        def _():
+            def one(c, _):
+                @pl.when(helping & (c > 0) & ready)
+                def _():
+                    pass_both(c - 1, 0)
+
+                @pl.when(helping & (c == pieces - 1) & soon)
+                def _():
+                    lax.fori_loop(0, soon_pieces, pass_both, 0)
+
+                @pl.when(from_up)
+                def _():
+                    take_left(d - 1, c)
+
+                @pl.when(jnp.logical_not(from_up))
+                def _():
+                    take_right(d - 1, c)
+
+                @pl.when(helping & (c < lead))
+                def _():
+                    help_step(c, 1)
+
+                @pl.when(helping & (c == pieces - 1))
+                def _():
+                    for j in range(2):
+                        lend_other(j, both.at[0, 0], left).wait_recv()
+                    over(help_step, 0, 0, pieces)
+
+                compute(b, 4, c, 1, (0, 1))
+                settle(b, 4, c, (0, 1))
+
+                @pl.when(helping & (c == pieces - 1))
+                def _():
+                    over(help_step, 1, lead, pieces)
+
+                @pl.when(late & (e == 4) & (c == min(1, pieces - 1)))
+                def _():
+                    early_compute(0, 0)
+                    early_compute(2, 0)
+                    early_settle(0, 0)
+                    early_settle(2, 0)
+
+                return 0
+
+            lax.fori_loop(0, pieces, one, 0)
+
+        @pl.when(is_last & (e == 4))
+        def _():
+            def rest(c, _):
+                take_right(0, c)
+                compute(p - 1, 4, c, 1, (0, 1))
+                settle(p - 1, 4, c, (0, 1))
+                return 0
+
+            lax.fori_loop(split, pieces, rest, 0)
+
+        return 0
+
+    lax.fori_loop(4, 2 * pairs - 1, block_step, 0)
 
     lent_to = is_last & (h == 0)
 
@@ -613,14 +623,9 @@
     def _():
         in_order(pass_on)
 
-    @pl.when(jnp.logical_not(lender | lent_to))
+    @pl.when(jnp.logical_not(lent_to | passed))
     def _():
-        def each(c, _):
-            pass_on(c, 0)
-            pass_on(c, 1)
-            return 0
-
-        lax.fori_loop(0, pieces, each, 0)
+        lax.fori_loop(jnp.where(ready, pieces - 1, jnp.where(soon, soon_pieces, 0)), pieces, pass_both, 0)
 
     for g in range(groups):
         def take_in(c, _):
@@ -690,10 +695,6 @@
         for j in range(2):
             lend_own(j).wait_send()
         lend_other(0, both.at[0, 0], left).wait_send()
-
-        @pl.when(jnp.logical_not(odd(0)) & (h != 0))
-        def _():
-            sent(lgot, s2_send.at[0])
 
     @pl.when(is_helper)
     def _():

time: 92.6 us -> 91 us (0.983)
  Pallas kernels: 90.2 us -> 88.2 us
    pallas_call x1, Pallas kernels: 90.2 us -> 88.2 us  [body(): pl.pallas_call(functools.partial(kernel, n_seq), out_shape=jax.ShapeDtype...]
where the time goes in v6:
time: 91 us; the launch traced here: 90.5 us
  Pallas kernels  88.2 us (97%)
  local copies, waits for them, and re-layouts  2.26 us (2%)
    pallas_call x1, Pallas kernels, body(): pl.pallas_call(functools.partial(kernel, n_seq), out_shape=jax.ShapeDtype...  88.2 us
    unnamed x1, local copies, waits for them, and re-layouts  2.26 us

profile of v6, /device:TPU:24, one launch (start us, length us, event | category | flops | bytes accessed | tf_op | source)
XLA Modules:
  0.0 90.5 jit_solution(9714639298627384049)
XLA Ops:
  0.0 88.2 %shard_map.55 = bf16[512,1024]{1,0:T(8,128)(2,1)} custom-call(s32[16]{0:T(128)} %lens_ref.1, bf16[512,1024]{1,0:T(8,128)(2,1)} %q_hbm.1, bf16[512,256]{1,0:T(8,128)(2,1)} %k_hbm.1, bf16[512,256]{1,0:T(8,128)(2,1)} %v_hbm.1, bf16[1024,512]{1,0:T(8,128)(2,1)} %w_hbm.1), custom_call_target="tpu_custom_call" | custom-call | tf_op jit(solution)/shard_map/pallas_call | solution.py:725
  88.2 2.3 %copy.7 = bf16[512,1024]{1,0:T(8,128)(2,1)} copy(bf16[512,1024]{1,0:T(8,128)(2,1)} %shard_map.55) | data formatting | bytes 2097152

commit v7 on v6

--- a/solution.py
+++ b/solution.py
@@ -13,6 +13,7 @@
 DH = 128
 MOST = 2048
 CHUNKS = 4
+OUT_PARTS = 4
 PIECE = 128
 MESH = pl.DeviceIdType.MESH
 
@@ -20,7 +21,7 @@
 def kernel(
     n_seq, lens_ref, q_hbm, k_hbm, v_hbm, w_hbm, out_hbm,
     q_ref, out_ref, kvbuf, wbuf, bias, vt, mx, sm, acc, both,
-    tmp, keep, sum1, sum2, give3, got3, lent, lsum1, lsum2, lgot,
+    tmp, keep, sum1, sum2, give3, lent, lsum1, lsum2, lgot,
     load_sem, out_sem, kvz_send, kvy_send, kv_recv, wl_send, wl_recv, wr_send, wr_recv,
     at_send, at_recv, s1_send, s1_recv, s2_send, s2_recv, s3_send, s3_recv,
     la_send, la_recv, l1_send, l1_recv, l2_send, l2_recv,
@@ -259,8 +260,11 @@
         piece = sum2.at[b, c, rows_of(side)]
         return copy(piece, piece, s2_send.at[b], s2_recv.at[b, c, side], s, far)
 
+    def columns(g, c, member):
+        return pl.ds(pl.multiple_of((2 * g + member) * wc + c * wcp, wcp), wcp)
+
     def third_copy(g, c):
-        return copy(give3.at[g, c], got3.at[g, c], s3_send.at[g], s3_recv.at[g, c], mate, h)
+        return copy(give3.at[g, c], out_ref.at[:, columns(g, c, m)], s3_send.at[g], s3_recv.at[g, c], mate, h)
 
     def odd(b):
         return lax.rem(b // groups + h, 2) == 1
@@ -509,9 +513,6 @@
             second_copy(0, c, side).wait_recv()
             for r in at:
                 store(r, (lgot[c, r].astype(jnp.float32) + sum2[0, c, r].astype(jnp.float32)).astype(jnp.bfloat16))
-
-    def columns(g, c, member):
-        return pl.ds(pl.multiple_of((2 * g + member) * wc + c * wcp, wcp), wcp)
 
     def place(g, c, r, member, value):
         at = pl.multiple_of(lax.rem(r, per_side) * part, part)
@@ -527,7 +528,7 @@
                 if side:
                     place(g, c, r, m, value)
                 else:
-                    give3[g, c, r] = value
+                    give3[g, c, pl.ds(r * part, part), :] = value
 
             result(g, c, side, store)
             if side:
@@ -630,8 +631,6 @@
     for g in range(groups):
         def take_in(c, _):
             third_copy(g, c).wait_recv()
-            for r in range(per_side):
-                place(g, c, r, 1 - m, got3[g, c, r])
             out_copy(g, c, 1 - m).start()
             return 0
 
@@ -707,6 +706,20 @@
         @pl.when(jnp.logical_not(odd(0)))
         def _():
             sent(lsum2, l2_send.at[0])
+
+
+def hand_over(src, dst, buf, sem):
+    part = src.shape[0] // OUT_PARTS
+    rows = [pl.ds(i * part, part) for i in range(OUT_PARTS)]
+    ins = [pltpu.make_async_copy(src.at[r], buf.at[r], sem.at[0, i]) for i, r in enumerate(rows)]
+    outs = [pltpu.make_async_copy(buf.at[r], dst.at[r], sem.at[1, i]) for i, r in enumerate(rows)]
+    for load in ins:
+        load.start()
+    for load, store in zip(ins, outs):
+        load.wait()
+        store.start()
+    for store in outs:
+        store.wait()
 
 
 def body(n_seq, queries, keys, values, doc_lengths, out_weight):
@@ -722,7 +735,7 @@
     slots = -(-(MOST - 1) // rows) + 1
     hbm = pl.BlockSpec(memory_space=pl.ANY)
     bf, f32, dma = jnp.bfloat16, jnp.float32, pltpu.SemaphoreType.DMA
-    return pl.pallas_call(
+    mixed = pl.pallas_call(
         functools.partial(kernel, n_seq),
         out_shape=jax.ShapeDtypeStruct((rows, wc * 2 * (pairs // 4)), bf),
         in_specs=[pl.BlockSpec(memory_space=pltpu.SMEM), hbm, hbm, hbm, hbm],
@@ -742,8 +755,7 @@
             pltpu.VMEM((groups, pieces, CHUNKS, part, wcp), f32),
             pltpu.VMEM((pairs, pieces, CHUNKS, part, wcp), bf),
             pltpu.VMEM((pairs, pieces, CHUNKS, part, wcp), bf),
-            pltpu.VMEM((groups, pieces, CHUNKS // 2, part, wcp), bf),
-            pltpu.VMEM((groups, pieces, CHUNKS // 2, part, wcp), bf),
+            pltpu.VMEM((groups, pieces, rows, wcp), bf),
             pltpu.VMEM((2, 2, rows, width // 2), bf),
             pltpu.VMEM((pieces, CHUNKS, part, wcp), bf),
             pltpu.VMEM((pieces, CHUNKS, part, wcp), bf),
@@ -758,6 +770,14 @@
             collective_id=0, has_side_effects=True, vmem_limit_bytes=56 * 1024 * 1024
         ),
     )(doc_lengths, queries, keys, values, out_weight)
+    return pl.pallas_call(
+        hand_over,
+        out_shape=jax.ShapeDtypeStruct(mixed.shape, mixed.dtype),
+        in_specs=[hbm],
+        out_specs=hbm,
+        scratch_shapes=[pltpu.VMEM(mixed.shape, mixed.dtype), dma((2, OUT_PARTS))],
+        compiler_params=pltpu.CompilerParams(vmem_limit_bytes=56 * 1024 * 1024),
+    )(mixed)
 
 
 def solution(mesh):

time: 91 us -> 90.7 us (level)
  local copies, waits for them, and re-layouts: 2.26 us -> 0 us
  Pallas kernels: 88.2 us -> 90.1 us
    unnamed x1 -> x0, local copies, waits for them, and re-layouts: 2.26 us -> none
    pallas_call x0 -> x1, Pallas kernels: none -> 1.98 us  [body(): pl.pallas_call(hand_over, out_shape=jax.ShapeDtypeStruct(mixed.shape, mix...]
where the time goes in v7:
time: 90.7 us; the launch traced here: 90.1 us
  Pallas kernels  90.1 us (99%)
    pallas_call x1, Pallas kernels, body(): pl.pallas_call(functools.partial(kernel, n_seq), out_shape=jax.ShapeDtype...  88.1 us
    pallas_call x1, Pallas kernels, body(): pl.pallas_call(hand_over, out_shape=jax.ShapeDtypeStruct(mixed.shape, mix...  1.98 us

profile of v7, /device:TPU:24, one launch (start us, length us, event | category | flops | bytes accessed | tf_op | source)
XLA Modules:
  0.0 90.1 jit_solution(10555052854518230394)
XLA Ops:
  0.0 88.1 %shard_map.55.src = bf16[512,1024]{1,0:T(8,128)(2,1)} custom-call(s32[16]{0:T(128)} %lens_ref.1, bf16[512,1024]{1,0:T(8,128)(2,1)} %q_hbm.1, bf16[512,256]{1,0:T(8,128)(2,1)} %k_hbm.1, bf16[512,256]{1,0:T(8,128)(2,1)} %v_hbm.1, bf16[1024,512]{1,0:T(8,128)(2,1)} %w_hbm.1), custom_call_target="tpu_custom_call" | custom-call | tf_op jit(solution)/shard_map/pallas_call | solution.py:738
  88.2 2.0 %shard_map.56 = bf16[512,1024]{1,0:T(8,128)(2,1)} custom-call(bf16[512,1024]{1,0:T(8,128)(2,1)} %shard_map.55.src), custom_call_target="tpu_custom_call" | custom-call | tf_op jit(solution)/shard_map/pallas_call | solution.py:773
